TPU v7x, 256 devices: a 4x2x16 block of a 4x16x16 slice. The times are simulated.
256 devices in a mesh: slides: 2 (over y), seq: 32 (over z, core), sub: 4 (over x).
Axes of the slice: x: 4, y: 2, z: 16, core: 2. Of those that a mesh axis runs over, the one named last changes fastest.
The devices are a block of a 4x16x16 slice.
Arguments:
- q_heads: bfloat16 [65536, 768], P(('slides', 'seq'), 'sub'), parts along dimension 0, may hold values from -8 to 8
- k_heads: bfloat16 [65536, 768], P(('slides', 'seq'), 'sub'), parts along dimension 0, may hold values from -8 to 8
- v_heads: bfloat16 [65536, 768], P(('slides', 'seq'), 'sub'), parts along dimension 0, may hold values from -6 to 6
- w_out: bfloat16 [768, 768], replicated, may hold values from -0.21875 to 0.21875
- offsets: int32 [2, 16], replicated, may hold values from 0 to 15, as said below
- valid: int32 [2], P('slides'), parts along dimension 0, may hold values from 31745 to 32768
Outputs:
- mixed: bfloat16 [65536, 768], P(('slides', 'seq'), 'sub'), parts along dimension 0
There are 2 independent parts, one for each index of `slides`. A program takes and returns all parts, laid end to end along the dimension named above; an argument that names none is the same for every part. Nothing has to cross between parts.
Inputs may be any that keep to these rules, and one draw needn't show every extreme that they name: `offsets`: row 0 lies below 4, row 1 below 16. Tiles at positions valid[0] and beyond are padding.
All inputs are finite; a program needn't handle non-finite values.
Results may differ from a plain program's by a relative error of at most 0.012.
Values may be sent and summed in bfloat16 or wider, within the bound.
No kernel may reach another device: no remote copies, remote signals or barrier semaphores. Data moves between devices by JAX's collectives and lax.ppermute only.
A program may use at most 64 MiB of HBM per device.

v0:
```python
import functools
import math

import jax
import jax.numpy as jnp
from jax import lax
from jax.experimental import pallas as pl
from jax.experimental.pallas import tpu as pltpu
from jax.sharding import PartitionSpec as P


HS = 48
R1 = 4
R2 = 16
LOG2_SCALE = HS ** (-0.5) * math.log2(math.e)
MASKED = -1e6

F32 = jnp.float32
BF16 = jnp.bfloat16


VMEM = pl.BlockSpec(memory_space=pltpu.VMEM)
SMEM = pl.BlockSpec(memory_space=pltpu.SMEM)


def lanes(width=128):
    return lax.broadcasted_iota(jnp.int32, (1, width), 1)


def head_lanes(h):
    lane = lanes(256)
    return ((lane >= h * HS) & (lane < (h + 1) * HS)) | (lane == 4 * HS + h)


def head_tile(h, tile):
    return head_lanes(h)[:, tile * 128 : (tile + 1) * 128]


def head_tile_all(h, tile):
    lane = lanes()
    if tile == 0:
        return (lane >= h * HS) & (lane < (h + 1) * HS)
    low = h * HS - 128
    return ((lane >= low) & (lane < low + HS) & (lane < 64)) | (lane == 64 + h) | (lane == 68 + h)


def attend(q, k, v, k_dims=(1,), v_dims=(0,)):
    scores = lax.dot_general(q, k, (((1,), k_dims), ((), ())), preferred_element_type=F32)
    peak = jnp.max(scores, axis=1, keepdims=True)
    probs = jnp.exp2((scores - peak) * LOG2_SCALE).astype(BF16)
    out = lax.dot_general(probs, v, (((1,), v_dims), ((), ())), preferred_element_type=F32)
    return peak * LOG2_SCALE, out


def prep_kernel(offs_hbm, k_hbm, v_hbm, mid_ref, wide_ref, k_ref, v_ref, offsets, kf, vf, tf, sems):
    copies = [
        pltpu.make_async_copy(source, target, sems.at[i])
        for i, (source, target) in enumerate(
            ((offs_hbm, offsets), (k_hbm, k_ref), (v_hbm, v_ref))
        )
    ]
    for copy in copies:
        copy.start()
    first_head = lax.axis_index("sub") * 4
    copies[1].wait()
    kf[...] = k_ref[:128, :].astype(F32).T
    copies[2].wait()
    vf[...] = v_ref[:128, :].astype(F32).T
    tf[...] = jnp.concatenate([k_ref[128:192, :], v_ref[128:192, :]], axis=0).astype(F32).T
    copies[0].wait()
    lane = lanes()
    for row, stride, out in ((0, R1, mid_ref), (1, R2, wide_ref)):
        count = out.shape[0]

        def pick(ref, h):
            return ref[pl.ds(offsets[row, first_head + h], count, stride=stride), :]

        for tile, ref in ((0, kf), (1, vf)):
            joined = jnp.where(lane < HS, pick(ref, 0), jnp.where(lane < 2 * HS, pick(ref, 1), pick(ref, 2)))
            out[:, tile * 128 : (tile + 1) * 128] = joined.astype(BF16)
        joined = jnp.where(lane % 64 < 16, pick(tf, 2), pick(tf, 3))
        out[:, 256:384] = joined.astype(BF16)


def near_kernel(valid, offs_hbm, q_ref, k_ref, v_ref, acc_ref, qm_ref, qw_ref, qa, ka, va, q0, q1, offsets, sem):
    rows = q_ref.shape[1]
    fetch = pltpu.make_async_copy(offs_hbm, offsets, sem)
    fetch.start()
    first_head = lax.axis_index("sub") * 4
    start = lax.axis_index("seq") * rows
    line = lax.broadcasted_iota(jnp.int32, (64, 1), 0)
    ones = jnp.broadcast_to(jnp.where(line < 4, 1.0, 0.0), (64, rows))
    q0[...] = q_ref[:128, :].astype(F32).T
    q1[...] = jnp.concatenate([q_ref[128:192, :].astype(F32), ones], axis=0).T
    qa[:, :128] = q0[...].astype(BF16)
    qa[:, 128:256] = q1[...].astype(BF16)
    position = start + lax.broadcasted_iota(jnp.int32, (1, rows), 1)
    dead = jnp.where(position < valid[0], 0.0, MASKED)
    ka[:192, :] = k_ref[...]
    ka[192:256, :] = jnp.where(line < 4, dead, 0.0).astype(BF16)
    va[:192, :] = v_ref[...]
    va[192:256, :] = ones.astype(BF16)
    fetch.wait()

    for row, stride, out in ((0, R1, qm_ref), (1, R2, qw_ref)):
        count = rows // stride
        for h in range(4):
            for tile, ref in ((0, q0), (1, q1)):
                picked = ref[pl.ds(offsets[row, first_head + h], count, stride=stride), :]
                picked = jnp.where(head_tile(h, tile), picked, 0.0)
                out[h * count : (h + 1) * count, tile * 128 : (tile + 1) * 128] = picked.astype(BF16)

    chunk = 512

    def step(i, carry):
        at = pl.ds(pl.multiple_of(i * chunk, chunk), chunk)
        q = qa[at, :]

        def score(h):
            qh = jnp.where(head_lanes(h), q, jnp.zeros((), BF16))
            return jnp.dot(qh, ka[...], preferred_element_type=F32)

        acc = jnp.zeros((chunk, 256), F32)
        later = score(0)
        for h in range(4):
            scores = later
            if h < 3:
                later = score(h + 1)
            peak = jnp.max(scores, axis=1, keepdims=True)
            probs = jnp.exp2((scores - peak) * LOG2_SCALE).astype(BF16)
            out = lax.dot_general(probs, va[...], (((1,), (1,)), ((), ())), preferred_element_type=F32)
            acc = jnp.where(head_lanes(h), out, acc)
            acc = jnp.where(lanes(256) == 4 * HS + 4 + h, peak * LOG2_SCALE, acc)
        acc_ref[0, at, :] = acc[:, :128]
        acc_ref[1, at, :] = acc[:, 128:]
        return carry

    lax.fori_loop(0, rows // chunk, step, 0)


def open_piece(piece, first, stride, offsets, row, valid, ka, va, at):
    count = piece.shape[0]
    first_head = lax.axis_index("sub") * 4
    lane = lanes()
    shift = jnp.zeros((1, 128), jnp.int32)
    for h in range(4):
        shift = jnp.where(lane == 64 + h, offsets[row, first_head + h], shift)
    position = first + stride * lax.broadcasted_iota(jnp.int32, (count, 128), 0) + shift
    mass = (lane >= 64) & (lane < 68)
    tail = piece[:, 256:384].astype(F32)
    dead = jnp.where(mass & (position >= valid[0]), MASKED, 0.0)
    ka[at, :128] = piece[:, :128]
    ka[at, 128:256] = jnp.where(lane < 64, tail, dead).astype(BF16)
    va[at, :128] = piece[:, 128:256]
    va[at, 128:256] = jnp.where(
        lane < 64, pltpu.roll(tail, 64, 1), jnp.where(mass, 1.0, 0.0)
    ).astype(BF16)


def merge(old, new, peak, h):
    before = old[1][:, 68 + h : 69 + h]
    top = jnp.maximum(before, peak)
    keep = jnp.exp2(before - top)
    add = jnp.exp2(peak - top)
    first = jnp.where(head_tile_all(h, 0), keep * old[0] + add * new[0], old[0]) if h < 3 else old[0]
    second = jnp.where(head_tile(h, 1), keep * old[1] + add * new[1], old[1])
    second = jnp.where(lanes() == 68 + h, top, second)
    return first, second


def normalised(first, second):
    lane = lanes()
    inv = [1.0 / second[:, 64 + h : 65 + h] for h in range(4)]
    one = first * jnp.where(lane < HS, inv[0], jnp.where(lane < 2 * HS, inv[1], inv[2]))
    two = second * jnp.where(lane < 16, inv[2], inv[3])
    return one, two


def packed(one, two):
    half = two.shape[0] // 2
    tail = jnp.where(lanes() < 64, two[:half], pltpu.roll(two[half:], 64, 1))
    return one.astype(BF16), tail.astype(BF16)


def middle_kernel(tok_rows, offsets, valid, acc_ref, qm_ref, own_ref, far_ref, swap_ref,
                  out_ref, accw_ref, ka, va, a0, a1):
    seq = lax.axis_index("seq")
    first_head = lax.axis_index("sub") * 4
    count = own_ref.shape[0]
    sources = (seq, seq ^ 2, seq ^ 1, seq ^ 3)
    pieces = (own_ref[...], far_ref[...], swap_ref[:count], swap_ref[count:])
    for i, (source, piece) in enumerate(zip(sources, pieces)):
        open_piece(piece, source * tok_rows, R1, offsets, 0, valid, ka, va, slice(i * count, (i + 1) * count))
    a0[...] = acc_ref[0]
    a1[...] = acc_ref[1]
    for h in range(4):
        peak, out = attend(qm_ref[h * count : (h + 1) * count], ka[...], va[...])
        at = pl.ds(offsets[0, first_head + h], count, stride=R1)
        first, second = merge((a0[at, :], a1[at, :]), (out[:, :128], out[:, 128:]), peak, h)
        if h < 3:
            a0[at, :] = first
        a1[at, :] = second
    wide = accw_ref.shape[1]
    first = jnp.zeros((wide, 128), F32)
    second = jnp.zeros((wide, 128), F32)
    for h in range(4):
        at = pl.ds(offsets[1, first_head + h], wide, stride=R2)
        here0, here1 = a0[at, :], a1[at, :]
        first = jnp.where(head_tile_all(h, 0), here0, first)
        second = jnp.where(head_tile_all(h, 1), here1, second)
        if h < 3:
            a0[at, :] = jnp.where(head_tile_all(h, 0), 0.0, here0)
        if h > 1:
            a1[at, :] = jnp.where(head_tile_all(h, 1) & (lanes() < 64), 0.0, here1)
    accw_ref[0] = first
    accw_ref[1] = second
    one, two = normalised(a0[...], a1[...])
    head, tail = packed(one, two)
    out_ref[: head.shape[0]] = head
    out_ref[head.shape[0] :] = tail


def gathered_from(n_chips, side, group):
    chip = lax.axis_index("seq") // 2
    ahead = 2 * side - 1
    four, eight = n_chips // 4, n_chips // 2
    pieces = []
    for step in ((0,), (-1, 1))[group]:
        pieces += [(step, side), (step + four * ahead, side), (step + four * ahead, 1 - side), (step + eight, side)]
    if group == 0:
        for step in (2 * ahead, (2 + four) * ahead):
            pieces += [(step, side), (step, 1 - side)]
    return [(lax.rem(chip + step + n_chips, n_chips), core) for step, core in pieces]


def wide_kernel(tok_rows, n_chips, plan, last, offsets, valid, qw_ref, accw_ref, *refs):
    keys, (out_ref, ka, va) = refs[: len(plan)], refs[len(plan) :]
    core = lax.rem(lax.axis_index("seq"), 2)
    count = qw_ref.shape[0] // 4
    base = 0
    for (group, swapped), ref in zip(plan, keys):
        for i, (chip, core_of) in enumerate(gathered_from(n_chips, 1 - core if swapped else core, group)):
            at = slice(base, base + count)
            first = (chip * 2 + core_of) * tok_rows
            open_piece(ref[i * count : (i + 1) * count], first, R2, offsets, 1, valid, ka, va, at)
            base += count
    peak, out = attend(qw_ref[...], ka[...], va[...])
    first, second = accw_ref[0], accw_ref[1]
    for h in range(4):
        rows = slice(h * count, (h + 1) * count)
        first, second = merge((first, second), (out[rows, :128], out[rows, 128:]), peak[rows], h)
    if not last:
        out_ref[0] = first
        out_ref[1] = second
        return
    head, tail = packed(*normalised(first, second))
    out_ref[:count] = head
    out_ref[count:] = tail


X_FROM = (0, -1, 1, 2)


def x_sources():
    sub, subs = lax.axis_index("sub"), lax.axis_size("sub")
    return [lax.rem(sub + step + subs, subs) for step in X_FROM]


def final_kernel(offsets, valid, w_ref, a0_ref, a1_ref, a2_ref, a3_ref, b0_ref, b1_ref, b2_ref, b3_ref,
                 out_ref, f0, f1, wp):
    cols, rows = out_ref.shape
    half, count, chunk = rows // 2, rows // R2, 256
    sources = x_sources()
    wp[...] = jnp.zeros(wp.shape, BF16)
    for i, source in enumerate(sources):
        at = pl.ds(pl.multiple_of(source * cols, cols), cols)
        for part in (0, 1):
            for low, high in ((0, 128), (128, cols)):
                piece = w_ref[at, low:high]
                wp[part, i * 256 : i * 256 + 128, low:high] = piece[:128]
                tail = i * 256 + 128 + part * 64
                wp[part, tail : tail + 64, low:high] = piece[128:]
    for part in (0, 1):
        for start in range(0, half, chunk):
            at = slice(part * half + start, part * half + start + chunk)
            tail = slice(rows + start, rows + start + chunk)
            x = jnp.concatenate(
                [piece for ref in (a0_ref, a1_ref, a2_ref, a3_ref) for piece in (ref[at], ref[tail])], axis=1
            )
            total = jnp.dot(x, wp[part], preferred_element_type=F32)
            f0[at, :] = total[:, :128]
            f1[at, :] = total[:, 128:]
    for i, ref in enumerate((b0_ref, b1_ref, b2_ref, b3_ref)):
        tail = ref[count:].astype(F32)
        second = jnp.concatenate([tail, pltpu.roll(tail, 64, 1)], axis=0)
        both = jnp.concatenate([ref[:count].astype(F32), second], axis=1)
        stacked = jnp.concatenate(
            [jnp.where(head_lanes(h) & (lanes(256) < 4 * HS), both, 0.0) for h in range(4)], axis=0
        )
        part = jnp.dot(stacked.astype(BF16), wp[0, i * 256 : (i + 1) * 256], preferred_element_type=F32)
        for h in range(4):
            at = pl.ds(offsets[1, sources[i] * 4 + h], count, stride=R2)
            rows_h = slice(h * count, (h + 1) * count)
            f0[at, :] = f0[at, :] + part[rows_h, :128]
            f1[at, :] = f1[at, :] + part[rows_h, 128:]
    position = lax.axis_index("seq") * rows + lax.broadcasted_iota(jnp.int32, (1, rows), 1)
    keep = position < valid[0]
    out_ref[:128, :] = jnp.where(keep, f0[...].T, 0.0).astype(BF16)
    out_ref[128:, :] = jnp.where(keep, f1[...].T[: cols - 128], 0.0).astype(BF16)


HBM = pl.BlockSpec(memory_space=pltpu.HBM)


def call(body, ins, outs, scratch, flops, limit=20):
    return pl.pallas_call(
        body,
        out_shape=[jax.ShapeDtypeStruct(s, d) for s, d in outs],
        in_specs=[{"s": SMEM, "v": VMEM, "a": HBM}[kind] for kind in ins],
        out_specs=[VMEM] * len(outs),
        scratch_shapes=[s if not isinstance(s, tuple) else pltpu.VMEM(*s) for s in scratch],
        cost_estimate=pl.CostEstimate(flops=int(flops), bytes_accessed=2 << 20, transcendentals=0),
        compiler_params=pltpu.CompilerParams(vmem_limit_bytes=limit << 20),
    )


def local(q_heads, k_heads, v_heads, w_out, offsets, valid):
    rows, cols = q_heads.shape
    sub = lax.axis_index("sub")
    n_seq = lax.axis_size("seq")
    n_sub = lax.axis_size("sub")
    n_chips = n_seq // 2
    mid, wide = rows // R1, rows // R2
    w_cols = lax.dynamic_slice_in_dim(w_out, sub * cols, cols, 1)

    def along_z(value, up, down):
        pairs = [(2 * z + c, 2 * ((z + (up, down)[c]) % n_chips) + c) for z in range(n_chips) for c in (0, 1)]
        return lax.ppermute(value, "seq", pairs)

    def flipped(value, mask):
        return lax.ppermute(value, "seq", [(i, i ^ mask) for i in range(n_seq)])

    def along_x(value, step):
        return lax.ppermute(value, "sub", [(i, (i + step) % n_sub) for i in range(n_sub)])

    smem_offsets = pltpu.SMEM(offsets.shape, jnp.int32)
    q_t, k_t, v_t = q_heads.T, k_heads.T, v_heads.T
    kv_mid, kv_wide = call(
        prep_kernel, "aaa",
        [((mid, 384), BF16), ((wide, 384), BF16)],
        [((cols, rows), BF16)] * 2 + [smem_offsets] + [((rows, 128), F32)] * 3 + [pltpu.SemaphoreType.DMA((3,))],
        2e8, 60,
    )(offsets, k_t, v_t)

    four = n_chips // 4
    kv_both = flipped(kv_wide, 1)
    far_mid = flipped(kv_mid, 2)
    own_pair = jnp.concatenate([kv_wide, kv_both], axis=0)
    far4 = along_z(own_pair, four, -four)
    acc, q_mid, q_wide = call(
        near_kernel, "savvv",
        [((2, rows, 128), F32), ((4 * mid, 256), BF16), ((4 * wide, 256), BF16)],
        [((rows, 256), BF16), ((256, rows), BF16), ((256, rows), BF16)] + [((rows, 128), F32)] * 2
        + [smem_offsets, pltpu.SemaphoreType.DMA],
        4e9, 28,
    )(valid, offsets, q_t, k_t, v_t)
    far_mid, acc = lax.optimization_barrier((far_mid, acc))

    swap_mid = flipped(jnp.concatenate([kv_mid, far_mid], axis=0), 1)
    far8 = along_z(far4[:wide], four, -four)
    mine = jnp.concatenate([kv_wide, far4, far8], axis=0)
    around2 = along_z(jnp.concatenate([own_pair, far4], axis=0), 2, -2)
    around_up = along_z(mine, 1, 1)
    around_down = along_z(mine, -1, -1)
    attn, acc_wide = call(
        functools.partial(middle_kernel, rows), "ssvvvvv",
        [((rows + rows // 2, 128), BF16), ((2, wide, 128), F32)],
        [((4 * mid, 256), BF16)] * 2 + [((rows, 128), F32)] * 2,
        1e9,
    )(offsets, valid, acc, q_mid, kv_mid, far_mid, swap_mid)
    attns = [along_x(attn, s) for s in (1, n_sub - 1, 2)]

    def wide_part(plan, acc_now, keys, last=False):
        n_keys = sum(k.shape[0] for k in keys)
        (result,) = call(
            functools.partial(wide_kernel, rows, n_chips, plan, last), "ssvv" + "v" * len(keys),
            [((wide + wide // 2, 128), BF16) if last else ((2, wide, 128), F32)],
            [((n_keys, 256), BF16)] * 2, 5e8,
        )(offsets, valid, q_wide, acc_now, *keys)
        return result

    early = jnp.concatenate([mine, around2], axis=0)
    early_other = flipped(early, 1)
    late = jnp.concatenate([around_up, around_down], axis=0)
    late_other = flipped(late, 1)
    acc_wide = wide_part(((0, False), (0, True)), acc_wide, (early, early_other))
    acc_wide = wide_part(((1, False),), acc_wide, (late,))
    attn_wide = wide_part(((1, True),), acc_wide, (late_other,), last=True)
    wides = [along_x(attn_wide, s) for s in (1, n_sub - 1, 2)]
    (out,) = call(
        final_kernel, "ssv" + "v" * 8, [((cols, rows), BF16)],
        [((rows, 128), F32)] * 2 + [((2, 4 * 256, 256), BF16)], 1e9,
    )(offsets, valid, w_cols, attn, *attns, attn_wide, *wides)
    return out.T


def solution(mesh):
    placed = (
        P(("slides", "seq"), "sub"),
        P(("slides", "seq"), "sub"),
        P(("slides", "seq"), "sub"),
        P(),
        P(),
        P("slides"),
    )


    return jax.shard_map(local, mesh=mesh, in_specs=placed, out_specs=P(("slides", "seq"), "sub"), check_vma=False)
```

profile of v0, /device:TPU:40, one launch (start us, length us, event | category | flops | bytes accessed | tf_op | source)
XLA Modules:
  0.0 94.6 jit_solution(8814931215370850636)
XLA Ops:
  0.0 0.0 copy-start
  0.0 2.4 %shard_map.64 = (bf16[256,384]{1,0:T(8,128)(2,1)}, bf16[64,384]{1,0:T(8,128)(2,1)}) custom-call(s32[2,16]{1,0:T(2,128)} %offsets.9, bf16[192,1024]{1,0:T(8,128)(2,1)} %bitcast.4, bf16[192,1024]{1,0:T(8,128)(2,1)} %bitcast.6), custom_call_target="tpu_custom_call" | custom-call | flops 200000000 | bytes 2097152 | tf_op jit(solution)/shard_map/pallas_call | solution.py:348
  2.4 2.9 %collective-permute-start = (bf16[256,384]{1,0:T(8,128)(2,1)}, bf16[256,384]{1,0:T(8,128)(2,1)S(1)}, u32[]{:S(2)}, u32[]{:S(2)}) collective-permute-start(bf16[256,384]{1,0:T(8,128)(2,1)} %get-tuple-element.14.own_ref), channel_id=1, source_target_pairs={{0,8},{4,12},{8,0},{12,4},{16,24},{20,28},{24,16},{28,20},{32,40},... | collective-permute-start | bytes 589832 | tf_op jit(solution)/shard_map/ppermute | solution.py:341
  5.3 0.0 collective-permute-start.5
  6.0 0.0 copy-start.1
  6.0 1.0 %copy-done.1 = bf16[1024,192]{0,1:T(8,128)(2,1)S(1)} copy-done((bf16[1024,192]{0,1:T(8,128)(2,1)S(1)}, bf16[1024,192]{0,1:T(8,128)(2,1)}, u32[]{:S(2)}) %copy-start.1) | copy-done | bytes 393240
  7.0 0.0 copy-start.2
  7.0 1.0 %copy-done.2 = bf16[1024,192]{0,1:T(8,128)(2,1)S(1)} copy-done((bf16[1024,192]{0,1:T(8,128)(2,1)S(1)}, bf16[1024,192]{0,1:T(8,128)(2,1)}, u32[]{:S(2)}) %copy-start.2) | copy-done | bytes 393240
  8.0 0.0 copy-start.4
  8.0 0.7 copy-done.4
  8.7 0.0 copy-start.6
  8.7 1.0 %copy-done.6 = bf16[1024,192]{0,1:T(8,128)(2,1)S(1)} copy-done((bf16[1024,192]{0,1:T(8,128)(2,1)S(1)}, bf16[1024,192]{0,1:T(8,128)(2,1)}, u32[]{:S(2)}) %copy-start.6) | copy-done | bytes 393240
  9.7 0.0 copy-start.7
  9.7 6.4 %shard_map.65 = (f32[2,1024,128]{2,1,0:T(8,128)S(1)}, bf16[1024,256]{1,0:T(8,128)(2,1)S(1)}, bf16[256,256]{1,0:T(8,128)(2,1)S(1)}) custom-call(s32[1]{0:T(128)S(6)} %copy.13.valid, s32[2,16]{1,0:T(2,128)S(1)} %copy-done.4, bf16[192,1024]{1,0:T(8,128)(2,1)S(1)} %bitcast.8, bf16[192,1024]{1,0:T(8,128)(2,1)S(1)} %bitcast.5, bf16[192,1024]{1,0:T(8,128)(2,1)S(1)} %bitcast.7), custom_call_target="tpu_custom_call" | custom-call | flops 4000000000 | bytes 2097152 | tf_op jit(solution)/shard_map/pallas_call | solution.py:360
  16.1 0.0 copy-start.3
  16.1 0.0 collective-permute-done.5
  16.1 0.0 copy-done.7
  16.1 10.7 %collective-permute-start.6 = (bf16[128,384]{1,0:T(8,128)(2,1)S(1)}, bf16[128,384]{1,0:T(8,128)(2,1)S(1)}, u32[]{:S(2)}, u32[]{:S(2)}) collective-permute-start(bf16[128,384]{1,0:T(8,128)(2,1)S(1)} %pad_maximum_fusion.2), channel_id=1, source_target_pairs={{0,32},{4,100},{8,40},{12,108},{16,48},{20,116},{24,56},{28,124},{... | collective-permute-start | bytes 294920 | tf_op jit(solution)/shard_map/ppermute | solution.py:338
  26.9 12.2 %collective-permute-done.6 = bf16[128,384]{1,0:T(8,128)(2,1)S(1)} collective-permute-done((bf16[128,384]{1,0:T(8,128)(2,1)S(1)}, bf16[128,384]{1,0:T(8,128)(2,1)S(1)}, u32[]{:S(2)}, u32[]{:S(2)}) %collective-permute-start.6) | collective-permute-done | bytes 98336 | tf_op jit(solution)/shard_map/ppermute | solution.py:338
  39.1 0.0 collective-permute-start.7
  39.2 3.5 %collective-permute-start.8 = (bf16[256,384]{1,0:T(8,128)(2,1)S(1)}, bf16[256,384]{1,0:T(8,128)(2,1)S(1)}, u32[]{:S(2)}, u32[]{:S(2)}) collective-permute-start(bf16[256,384]{1,0:T(8,128)(2,1)S(1)} %pad_maximum_fusion.1), channel_id=1, source_target_pairs={{0,16},{4,116},{8,24},{12,124},{16,32},{20,4},{24,40},{28,12},{32,... | collective-permute-start | bytes 589832 | tf_op jit(solution)/shard_map/ppermute | solution.py:338
  42.7 6.8 %collective-permute-done.7 = bf16[64,384]{1,0:T(8,128)(2,1)S(1)} collective-permute-done((bf16[64,384]{1,0:T(8,128)(2,1)S(1)}, bf16[64,384]{1,0:T(8,128)(2,1)S(1)}, u32[]{:S(2)}, u32[]{:S(2)}) %collective-permute-start.7) | collective-permute-done | bytes 49184 | tf_op jit(solution)/shard_map/ppermute | solution.py:338
  49.6 0.1 collective-permute-start.10
  49.7 6.2 %collective-permute-start.11 = (bf16[256,384]{1,0:T(8,128)(2,1)S(1)}, bf16[256,384]{1,0:T(8,128)(2,1)S(1)}, u32[]{:S(2)}, u32[]{:S(2)}) collective-permute-start(bf16[256,384]{1,0:T(8,128)(2,1)S(1)} %get-tuple-element.25), channel_id=1, source_target_pairs={{0,120},{4,124},{8,0},{12,4},{16,8},{20,12},{24,16},{28,20},{32,24... | collective-permute-start | bytes 589832 | tf_op jit(solution)/shard_map/ppermute | solution.py:338
  56.0 0.0 collective-permute-done.far_ref
  56.0 0.0 copy-done.3
  56.0 0.1 collective-permute-start.1
  56.2 0.0 collective-permute-done.8
  56.2 0.6 collective-permute-start.9
  56.8 2.7 %collective-permute-done.10 = bf16[256,384]{1,0:T(8,128)(2,1)S(1)} collective-permute-done((bf16[256,384]{1,0:T(8,128)(2,1)S(1)}, bf16[256,384]{1,0:T(8,128)(2,1)S(1)}, u32[]{:S(2)}, u32[]{:S(2)}) %collective-permute-start.10) | collective-permute-done | bytes 196640 | tf_op jit(solution)/shard_map/ppermute | solution.py:338
  59.5 0.0 collective-permute-done.11
  59.6 0.3 collective-permute-start.12
  59.9 0.0 collective-permute-done.1.swap_ref
  59.9 3.6 %shard_map.66 = (bf16[1536,128]{1,0:T(8,128)(2,1)S(1)}, f32[2,64,128]{2,1,0:T(8,128)S(1)}) custom-call(s32[2,16]{1,0:T(2,128)S(1)} %copy-done.4, s32[1]{0:T(128)S(6)} %copy.13.valid, f32[2,1024,128]{2,1,0:T(8,128)S(1)} %get-tuple-element.16.acc_ref, bf16[1024,256]{1,0:T(8,128)(2,1)S(1)} %get-tuple-element.17.qm_ref, bf16[256,384]{1,0:T(8,128)(2,1)S(1)} %copy-done.3, ...), custom_call_target="tpu_custom_call" | custom-call | flops 1000000000 | bytes 2097152 | tf_op jit(solution)/shard_map/pallas_call | solution.py:375
  63.6 1.8 %collective-permute-start.2 = (bf16[1536,128]{1,0:T(8,128)(2,1)S(1)}, bf16[1536,128]{1,0:T(8,128)(2,1)S(1)}, u32[]{:S(2)}, u32[]{:S(2)}) collective-permute-start(bf16[1536,128]{1,0:T(8,128)(2,1)S(1)} %get-tuple-element.19.a0_ref), channel_id=1, source_target_pairs={{0,1},{1,2},{2,3},{3,0},{4,5},{5,6},{6,7},{7,4},{8,9},{9,10},{10,1... | collective-permute-start | bytes 1179656 | tf_op jit(solution)/shard_map/ppermute | solution.py:344
  65.4 1.6 %collective-permute-start.3 = (bf16[1536,128]{1,0:T(8,128)(2,1)S(1)}, bf16[1536,128]{1,0:T(8,128)(2,1)S(1)}, u32[]{:S(2)}, u32[]{:S(2)}) collective-permute-start(bf16[1536,128]{1,0:T(8,128)(2,1)S(1)} %get-tuple-element.19.a0_ref), channel_id=1, source_target_pairs={{0,3},{1,0},{2,1},{3,2},{4,7},{5,4},{6,5},{7,6},{8,11},{9,8},{10,9... | collective-permute-start | bytes 1179656 | tf_op jit(solution)/shard_map/ppermute | solution.py:344
  67.0 2.0 %collective-permute-start.4 = (bf16[1536,128]{1,0:T(8,128)(2,1)S(1)}, bf16[1536,128]{1,0:T(8,128)(2,1)S(1)}, u32[]{:S(2)}, u32[]{:S(2)}) collective-permute-start(bf16[1536,128]{1,0:T(8,128)(2,1)S(1)} %get-tuple-element.19.a0_ref), channel_id=1, source_target_pairs={{0,2},{1,3},{2,0},{3,1},{4,6},{5,7},{6,4},{7,5},{8,10},{9,11},{10,... | collective-permute-start | bytes 1179656 | tf_op jit(solution)/shard_map/ppermute | solution.py:344
  69.0 0.0 collective-permute-done.9.refs_1_
  69.0 1.7 %shard_map.67.accw_ref = f32[2,64,128]{2,1,0:T(8,128)S(1)} custom-call(s32[2,16]{1,0:T(2,128)S(1)} %copy-done.4, s32[1]{0:T(128)S(6)} %copy.13.valid, bf16[256,256]{1,0:T(8,128)(2,1)S(1)} %get-tuple-element.20.qw_ref, f32[2,64,128]{2,1,0:T(8,128)S(1)} %get-tuple-element.21.accw_ref, bf16[512,384]{1,0:T(8,128)(2,1)S(1)} %constant_dynamic-update-slice_fusion.refs_0_, ...), custom_call_target="tpu_custom_call" | custom-call | flops 500000000 | bytes 2097152 | tf_op jit(solution)/shard_map/pallas_call | solution.py:385
  70.8 1.4 %shard_map.68.accw_ref = f32[2,64,128]{2,1,0:T(8,128)S(1)} custom-call(s32[2,16]{1,0:T(2,128)S(1)} %copy-done.4, s32[1]{0:T(128)S(6)} %copy.13.valid, bf16[256,256]{1,0:T(8,128)(2,1)S(1)} %get-tuple-element.20.qw_ref, f32[2,64,128]{2,1,0:T(8,128)S(1)} %shard_map.67.accw_ref, bf16[512,384]{1,0:T(8,128)(2,1)S(1)} %constant_dynamic-update-slice_fusion.7.refs_0_), custom_call_target="tpu_custom_call" | custom-call | flops 500000000 | bytes 2097152 | tf_op jit(solution)/shard_map/pallas_call | solution.py:385
  72.2 0.0 copy-start.5
  72.2 0.0 collective-permute-done.12.refs_0_
  72.3 1.6 %shard_map.69.b0_ref = bf16[96,128]{1,0:T(8,128)(2,1)S(1)} custom-call(s32[2,16]{1,0:T(2,128)S(1)} %copy-done.4, s32[1]{0:T(128)S(6)} %copy.13.valid, bf16[256,256]{1,0:T(8,128)(2,1)S(1)} %get-tuple-element.20.qw_ref, f32[2,64,128]{2,1,0:T(8,128)S(1)} %shard_map.68.accw_ref, bf16[512,384]{1,0:T(8,128)(2,1)S(1)} %collective-permute-done.12.refs_0_), custom_call_target="tpu_custom_call" | custom-call | flops 500000000 | bytes 2097152 | tf_op jit(solution)/shard_map/pallas_call | solution.py:385
  73.9 0.8 collective-permute-start.13
  74.7 2.5 %collective-permute-start.14 = (bf16[96,128]{1,0:T(8,128)(2,1)S(1)}, bf16[96,128]{1,0:T(8,128)(2,1)S(1)}, u32[]{:S(2)}, u32[]{:S(2)}) collective-permute-start(bf16[96,128]{1,0:T(8,128)(2,1)S(1)} %shard_map.69.b0_ref), channel_id=1, source_target_pairs={{0,3},{1,0},{2,1},{3,2},{4,7},{5,4},{6,5},{7,6},{8,11},{9,8},{10,9... | collective-permute-start | bytes 73736 | tf_op jit(solution)/shard_map/ppermute | solution.py:344
  77.2 9.0 %collective-permute-done.13.b1_ref = bf16[96,128]{1,0:T(8,128)(2,1)S(1)} collective-permute-done((bf16[96,128]{1,0:T(8,128)(2,1)S(1)}, bf16[96,128]{1,0:T(8,128)(2,1)S(1)}, u32[]{:S(2)}, u32[]{:S(2)}) %collective-permute-start.13) | collective-permute-done | bytes 24608 | tf_op jit(solution)/shard_map/ppermute | solution.py:344
  86.2 1.2 %collective-permute-start.15 = (bf16[96,128]{1,0:T(8,128)(2,1)S(1)}, bf16[96,128]{1,0:T(8,128)(2,1)S(1)}, u32[]{:S(2)}, u32[]{:S(2)}) collective-permute-start(bf16[96,128]{1,0:T(8,128)(2,1)S(1)} %shard_map.69.b0_ref), channel_id=1, source_target_pairs={{0,2},{1,3},{2,0},{3,1},{4,6},{5,7},{6,4},{7,5},{8,10},{9,11},{10,... | collective-permute-start | bytes 73736 | tf_op jit(solution)/shard_map/ppermute | solution.py:344
  87.4 0.0 copy-done
  87.4 0.2 constant_dynamic-slice_fusion.w_ref
  87.6 0.0 collective-permute-done.14.b2_ref
  87.6 3.9 %collective-permute-done.15.b3_ref = bf16[96,128]{1,0:T(8,128)(2,1)S(1)} collective-permute-done((bf16[96,128]{1,0:T(8,128)(2,1)S(1)}, bf16[96,128]{1,0:T(8,128)(2,1)S(1)}, u32[]{:S(2)}, u32[]{:S(2)}) %collective-permute-start.15) | collective-permute-done | bytes 24608 | tf_op jit(solution)/shard_map/ppermute | solution.py:344
  91.5 0.0 collective-permute-done.2.a1_ref
  91.5 0.0 collective-permute-done.3.a2_ref
  91.5 0.0 collective-permute-done.4.a3_ref
  91.6 0.0 copy-done.5
  91.6 3.0 %shard_map.70 = bf16[192,1024]{1,0:T(8,128)(2,1)} custom-call(s32[2,16]{1,0:T(2,128)S(1)} %copy-done.5, s32[1]{0:T(128)S(6)} %copy.13.valid, bf16[768,192]{1,0:T(8,128)(2,1)S(1)} %constant_dynamic-slice_fusion.w_ref, bf16[1536,128]{1,0:T(8,128)(2,1)S(1)} %get-tuple-element.19.a0_ref, bf16[1536,128]{1,0:T(8,128)(2,1)S(1)} %collective-permute-done.2.a1_ref, ...), custom_call_target="tpu_custom_call" | custom-call | flops 1000000000 | bytes 2097152 | tf_op jit(solution)/shard_map/pallas_call | solution.py:400
  (10 shorter events, 0.2 us)
Async XLA Ops:
  0.0 87.4 %copy-start = (bf16[768,768]{1,0:T(8,128)(2,1)S(1)}, bf16[768,768]{1,0:T(8,128)(2,1)}, u32[]{:S(2)}) copy-start(bf16[768,768]{1,0:T(8,128)(2,1)} %param.9) | copy-start | bytes 3538948
  2.4 53.6 %collective-permute-start = (bf16[256,384]{1,0:T(8,128)(2,1)}, bf16[256,384]{1,0:T(8,128)(2,1)S(1)}, u32[]{:S(2)}, u32[]{:S(2)}) collective-permute-start(bf16[256,384]{1,0:T(8,128)(2,1)} %get-tuple-element.14.own_ref), channel_id=1, source_target_pairs={{0,8},{4,12},{8,0},{12,4},{16,24},{20,28},{24,16},{28,20},{32,40},... | collective-permute-start | bytes 589832 | tf_op jit(solution)/shard_map/ppermute | solution.py:341
  5.3 10.8 %collective-permute-start.5 = (bf16[64,384]{1,0:T(8,128)(2,1)}, bf16[64,384]{1,0:T(8,128)(2,1)S(1)}, u32[]{:S(2)}, u32[]{:S(2)}) collective-permute-start(bf16[64,384]{1,0:T(8,128)(2,1)} %get-tuple-element.22), channel_id=1, source_target_pairs={{0,4},{4,0},{8,12},{12,8},{16,20},{20,16},{24,28},{28,24},{32,36},... | collective-permute-start | bytes 147464 | tf_op jit(solution)/shard_map/ppermute | solution.py:341
  6.0 1.0 %copy-start.1 = (bf16[1024,192]{0,1:T(8,128)(2,1)S(1)}, bf16[1024,192]{0,1:T(8,128)(2,1)}, u32[]{:S(2)}) copy-start(bf16[1024,192]{0,1:T(8,128)(2,1)} %param.7) | copy-start | bytes 1179652
  7.0 1.0 %copy-start.2 = (bf16[1024,192]{0,1:T(8,128)(2,1)S(1)}, bf16[1024,192]{0,1:T(8,128)(2,1)}, u32[]{:S(2)}) copy-start(bf16[1024,192]{0,1:T(8,128)(2,1)} %param.8) | copy-start | bytes 1179652
  8.0 0.7 copy-start.4
  8.7 1.0 %copy-start.6 = (bf16[1024,192]{0,1:T(8,128)(2,1)S(1)}, bf16[1024,192]{0,1:T(8,128)(2,1)}, u32[]{:S(2)}) copy-start(bf16[1024,192]{0,1:T(8,128)(2,1)} %param.6) | copy-start | bytes 1179652
  9.7 6.4 %copy-start.7 = (bf16[64,384]{1,0:T(8,128)(2,1)S(1)}, bf16[64,384]{1,0:T(8,128)(2,1)}, u32[]{:S(2)}) copy-start(bf16[64,384]{1,0:T(8,128)(2,1)} %get-tuple-element.22) | copy-start | bytes 147460
  16.1 39.9 %copy-start.3 = (bf16[256,384]{1,0:T(8,128)(2,1)S(1)}, bf16[256,384]{1,0:T(8,128)(2,1)}, u32[]{:S(2)}) copy-start(bf16[256,384]{1,0:T(8,128)(2,1)} %get-tuple-element.14.own_ref) | copy-start | bytes 589828
  16.1 23.0 %collective-permute-start.6 = (bf16[128,384]{1,0:T(8,128)(2,1)S(1)}, bf16[128,384]{1,0:T(8,128)(2,1)S(1)}, u32[]{:S(2)}, u32[]{:S(2)}) collective-permute-start(bf16[128,384]{1,0:T(8,128)(2,1)S(1)} %pad_maximum_fusion.2), channel_id=1, source_target_pairs={{0,32},{4,100},{8,40},{12,108},{16,48},{20,116},{24,56},{28,124},{... | collective-permute-start | bytes 294920 | tf_op jit(solution)/shard_map/ppermute | solution.py:338
  39.1 10.5 %collective-permute-start.7 = (bf16[64,384]{1,0:T(8,128)(2,1)S(1)}, bf16[64,384]{1,0:T(8,128)(2,1)S(1)}, u32[]{:S(2)}, u32[]{:S(2)}) collective-permute-start(bf16[64,384]{1,0:T(8,128)(2,1)S(1)} %slice.4), channel_id=1, source_target_pairs={{0,32},{4,100},{8,40},{12,108},{16,48},{20,116},{24,56},{28,124},{... | collective-permute-start | bytes 147464 | tf_op jit(solution)/shard_map/ppermute | solution.py:338
  39.2 17.0 %collective-permute-start.8 = (bf16[256,384]{1,0:T(8,128)(2,1)S(1)}, bf16[256,384]{1,0:T(8,128)(2,1)S(1)}, u32[]{:S(2)}, u32[]{:S(2)}) collective-permute-start(bf16[256,384]{1,0:T(8,128)(2,1)S(1)} %pad_maximum_fusion.1), channel_id=1, source_target_pairs={{0,16},{4,116},{8,24},{12,124},{16,32},{20,4},{24,40},{28,12},{32,... | collective-permute-start | bytes 589832 | tf_op jit(solution)/shard_map/ppermute | solution.py:338
  49.6 9.9 %collective-permute-start.10 = (bf16[256,384]{1,0:T(8,128)(2,1)S(1)}, bf16[256,384]{1,0:T(8,128)(2,1)S(1)}, u32[]{:S(2)}, u32[]{:S(2)}) collective-permute-start(bf16[256,384]{1,0:T(8,128)(2,1)S(1)} %get-tuple-element.25), channel_id=1, source_target_pairs={{0,8},{4,12},{8,16},{12,20},{16,24},{20,28},{24,32},{28,36},{32,40... | collective-permute-start | bytes 589832 | tf_op jit(solution)/shard_map/ppermute | solution.py:338
  49.7 9.8 %collective-permute-start.11 = (bf16[256,384]{1,0:T(8,128)(2,1)S(1)}, bf16[256,384]{1,0:T(8,128)(2,1)S(1)}, u32[]{:S(2)}, u32[]{:S(2)}) collective-permute-start(bf16[256,384]{1,0:T(8,128)(2,1)S(1)} %get-tuple-element.25), channel_id=1, source_target_pairs={{0,120},{4,124},{8,0},{12,4},{16,8},{20,12},{24,16},{28,20},{32,24... | collective-permute-start | bytes 589832 | tf_op jit(solution)/shard_map/ppermute | solution.py:338
  56.0 3.9 %collective-permute-start.1 = (bf16[512,384]{1,0:T(8,128)(2,1)S(1)}, bf16[512,384]{1,0:T(8,128)(2,1)S(1)}, u32[]{:S(2)}, u32[]{:S(2)}) collective-permute-start(bf16[512,384]{1,0:T(8,128)(2,1)S(1)} %pad_maximum_fusion), channel_id=1, source_target_pairs={{0,4},{4,0},{8,12},{12,8},{16,20},{20,16},{24,28},{28,24},{32,36},... | collective-permute-start | bytes 1179656 | tf_op jit(solution)/shard_map/ppermute | solution.py:341
  56.2 12.8 %collective-permute-start.9 = (bf16[512,384]{1,0:T(8,128)(2,1)S(1)}, bf16[512,384]{1,0:T(8,128)(2,1)S(1)}, u32[]{:S(2)}, u32[]{:S(2)}) collective-permute-start(bf16[512,384]{1,0:T(8,128)(2,1)S(1)} %constant_dynamic-update-slice_fusion.refs_0_), channel_id=1, source_target_pairs={{0,4},{4,0},{8,12},{12,8},{16,20},{20,16},{24,28},{28,24},{32,36},... | collective-permute-start | bytes 1179656 | tf_op jit(solution)/shard_map/ppermute | solution.py:341
  59.6 12.7 %collective-permute-start.12 = (bf16[512,384]{1,0:T(8,128)(2,1)S(1)}, bf16[512,384]{1,0:T(8,128)(2,1)S(1)}, u32[]{:S(2)}, u32[]{:S(2)}) collective-permute-start(bf16[512,384]{1,0:T(8,128)(2,1)S(1)} %constant_dynamic-update-slice_fusion.7.refs_0_), channel_id=1, source_target_pairs={{0,4},{4,0},{8,12},{12,8},{16,20},{20,16},{24,28},{28,24},{32,36},... | collective-permute-start | bytes 1179656 | tf_op jit(solution)/shard_map/ppermute | solution.py:341
  63.6 28.0 %collective-permute-start.2 = (bf16[1536,128]{1,0:T(8,128)(2,1)S(1)}, bf16[1536,128]{1,0:T(8,128)(2,1)S(1)}, u32[]{:S(2)}, u32[]{:S(2)}) collective-permute-start(bf16[1536,128]{1,0:T(8,128)(2,1)S(1)} %get-tuple-element.19.a0_ref), channel_id=1, source_target_pairs={{0,1},{1,2},{2,3},{3,0},{4,5},{5,6},{6,7},{7,4},{8,9},{9,10},{10,1... | collective-permute-start | bytes 1179656 | tf_op jit(solution)/shard_map/ppermute | solution.py:344
  65.4 26.2 %collective-permute-start.3 = (bf16[1536,128]{1,0:T(8,128)(2,1)S(1)}, bf16[1536,128]{1,0:T(8,128)(2,1)S(1)}, u32[]{:S(2)}, u32[]{:S(2)}) collective-permute-start(bf16[1536,128]{1,0:T(8,128)(2,1)S(1)} %get-tuple-element.19.a0_ref), channel_id=1, source_target_pairs={{0,3},{1,0},{2,1},{3,2},{4,7},{5,4},{6,5},{7,6},{8,11},{9,8},{10,9... | collective-permute-start | bytes 1179656 | tf_op jit(solution)/shard_map/ppermute | solution.py:344
  67.0 24.5 %collective-permute-start.4 = (bf16[1536,128]{1,0:T(8,128)(2,1)S(1)}, bf16[1536,128]{1,0:T(8,128)(2,1)S(1)}, u32[]{:S(2)}, u32[]{:S(2)}) collective-permute-start(bf16[1536,128]{1,0:T(8,128)(2,1)S(1)} %get-tuple-element.19.a0_ref), channel_id=1, source_target_pairs={{0,2},{1,3},{2,0},{3,1},{4,6},{5,7},{6,4},{7,5},{8,10},{9,11},{10,... | collective-permute-start | bytes 1179656 | tf_op jit(solution)/shard_map/ppermute | solution.py:344
  72.2 19.3 %copy-start.5 = (s32[2,16]{1,0:T(2,128)S(1)}, s32[2,16]{1,0:T(2,128)}, u32[]{:S(2)}) copy-start(s32[2,16]{1,0:T(2,128)} %offsets.9) | copy-start | bytes 388
  73.9 12.3 %collective-permute-start.13 = (bf16[96,128]{1,0:T(8,128)(2,1)S(1)}, bf16[96,128]{1,0:T(8,128)(2,1)S(1)}, u32[]{:S(2)}, u32[]{:S(2)}) collective-permute-start(bf16[96,128]{1,0:T(8,128)(2,1)S(1)} %shard_map.69.b0_ref), channel_id=1, source_target_pairs={{0,1},{1,2},{2,3},{3,0},{4,5},{5,6},{6,7},{7,4},{8,9},{9,10},{10,1... | collective-permute-start | bytes 73736 | tf_op jit(solution)/shard_map/ppermute | solution.py:344
  74.7 12.9 %collective-permute-start.14 = (bf16[96,128]{1,0:T(8,128)(2,1)S(1)}, bf16[96,128]{1,0:T(8,128)(2,1)S(1)}, u32[]{:S(2)}, u32[]{:S(2)}) collective-permute-start(bf16[96,128]{1,0:T(8,128)(2,1)S(1)} %shard_map.69.b0_ref), channel_id=1, source_target_pairs={{0,3},{1,0},{2,1},{3,2},{4,7},{5,4},{6,5},{7,6},{8,11},{9,8},{10,9... | collective-permute-start | bytes 73736 | tf_op jit(solution)/shard_map/ppermute | solution.py:344
  86.2 5.3 %collective-permute-start.15 = (bf16[96,128]{1,0:T(8,128)(2,1)S(1)}, bf16[96,128]{1,0:T(8,128)(2,1)S(1)}, u32[]{:S(2)}, u32[]{:S(2)}) collective-permute-start(bf16[96,128]{1,0:T(8,128)(2,1)S(1)} %shard_map.69.b0_ref), channel_id=1, source_target_pairs={{0,2},{1,3},{2,0},{3,1},{4,6},{5,7},{6,4},{7,5},{8,10},{9,11},{10,... | collective-permute-start | bytes 73736 | tf_op jit(solution)/shard_map/ppermute | solution.py:344
where the time goes:
time: 94.8 us; the launch traced here: 94.6 us
  waiting for transfers between devices  34.7 us (37%)
  starting transfers between devices  34.6 us (36%)
  Pallas kernels  20.3 us (21%)
  local copies, waits for them, and re-layouts  4.01 us (4%)
    ppermute x5, waiting for transfers between devices, along_z(): return lax.ppermute(value, 'seq', pairs)  21.7 us
    ppermute x5, starting transfers between devices, along_z(): return lax.ppermute(value, 'seq', pairs)  20.7 us
    ppermute x6, waiting for transfers between devices, along_x(): lax.ppermute(value, 'sub', [(i, (i + step) % n_sub) for i in range(n_sub)])  12.9 us
    ppermute x6, starting transfers between devices, along_x(): lax.ppermute(value, 'sub', [(i, (i + step) % n_sub) for i in range(n_sub)])  10 us
    pallas_call x1, Pallas kernels, local(): call(near_kernel, 'savvv', [((2, rows, 128), F32), ((4 * mid, 256), BF16)...  6.41 us
    pallas_call x3, Pallas kernels, wide_part(): call(functools.partial(wide_kernel, rows, n_chips, plan, last), 'ssvv' +...  4.81 us
    ppermute x5, starting transfers between devices, flipped(): return lax.ppermute(value, 'seq', [(i, i ^ mask) for i in range(n_seq)])  3.96 us
    unnamed x19, local copies, waits for them, and re-layouts  3.74 us
  transfers between devices with their start and end apart: 16, of which 5 were waited for; matrix products, arithmetic and copies ran while one was open for 0% of the time, Pallas kernels for 16%

commit v1 on v0

--- a/solution.py
+++ b/solution.py
@@ -42,6 +42,10 @@
         return (lane >= h * HS) & (lane < (h + 1) * HS)
     low = h * HS - 128
     return ((lane >= low) & (lane < low + HS) & (lane < 64)) | (lane == 64 + h) | (lane == 68 + h)
+
+
+def offset_of(code, row, h):
+    return (code[0] >> (6 * h + 2 * row)) & (R1 - 1, R2 - 1)[row]
 
 
 def attend(q, k, v, k_dims=(1,), v_dims=(0,)):
@@ -82,11 +86,8 @@
         out[:, 256:384] = joined.astype(BF16)
 
 
-def near_kernel(valid, offs_hbm, q_ref, k_ref, v_ref, acc_ref, qm_ref, qw_ref, qa, ka, va, q0, q1, offsets, sem):
+def near_kernel(code, valid, q_ref, k_ref, v_ref, acc_ref, qm_ref, qw_ref, qa, ka, va, q0, q1):
     rows = q_ref.shape[1]
-    fetch = pltpu.make_async_copy(offs_hbm, offsets, sem)
-    fetch.start()
-    first_head = lax.axis_index("sub") * 4
     start = lax.axis_index("seq") * rows
     line = lax.broadcasted_iota(jnp.int32, (64, 1), 0)
     ones = jnp.broadcast_to(jnp.where(line < 4, 1.0, 0.0), (64, rows))
@@ -100,13 +101,12 @@
     ka[192:256, :] = jnp.where(line < 4, dead, 0.0).astype(BF16)
     va[:192, :] = v_ref[...]
     va[192:256, :] = ones.astype(BF16)
-    fetch.wait()
 
     for row, stride, out in ((0, R1, qm_ref), (1, R2, qw_ref)):
         count = rows // stride
         for h in range(4):
             for tile, ref in ((0, q0), (1, q1)):
-                picked = ref[pl.ds(offsets[row, first_head + h], count, stride=stride), :]
+                picked = ref[pl.ds(offset_of(code, row, h), count, stride=stride), :]
                 picked = jnp.where(head_tile(h, tile), picked, 0.0)
                 out[h * count : (h + 1) * count, tile * 128 : (tile + 1) * 128] = picked.astype(BF16)
 
@@ -138,13 +138,12 @@
     lax.fori_loop(0, rows // chunk, step, 0)
 
 
-def open_piece(piece, first, stride, offsets, row, valid, ka, va, at):
+def open_piece(piece, first, stride, code, row, valid, ka, va, at):
     count = piece.shape[0]
-    first_head = lax.axis_index("sub") * 4
     lane = lanes()
     shift = jnp.zeros((1, 128), jnp.int32)
     for h in range(4):
-        shift = jnp.where(lane == 64 + h, offsets[row, first_head + h], shift)
+        shift = jnp.where(lane == 64 + h, offset_of(code, row, h), shift)
     position = first + stride * lax.broadcasted_iota(jnp.int32, (count, 128), 0) + shift
     mass = (lane >= 64) & (lane < 68)
     tail = piece[:, 256:384].astype(F32)
@@ -182,20 +181,19 @@
     return one.astype(BF16), tail.astype(BF16)
 
 
-def middle_kernel(tok_rows, offsets, valid, acc_ref, qm_ref, own_ref, far_ref, swap_ref,
+def middle_kernel(tok_rows, code, valid, acc_ref, qm_ref, own_ref, far_ref, swap_ref,
                   out_ref, accw_ref, ka, va, a0, a1):
     seq = lax.axis_index("seq")
-    first_head = lax.axis_index("sub") * 4
     count = own_ref.shape[0]
     sources = (seq, seq ^ 2, seq ^ 1, seq ^ 3)
     pieces = (own_ref[...], far_ref[...], swap_ref[:count], swap_ref[count:])
     for i, (source, piece) in enumerate(zip(sources, pieces)):
-        open_piece(piece, source * tok_rows, R1, offsets, 0, valid, ka, va, slice(i * count, (i + 1) * count))
+        open_piece(piece, source * tok_rows, R1, code, 0, valid, ka, va, slice(i * count, (i + 1) * count))
     a0[...] = acc_ref[0]
     a1[...] = acc_ref[1]
     for h in range(4):
         peak, out = attend(qm_ref[h * count : (h + 1) * count], ka[...], va[...])
-        at = pl.ds(offsets[0, first_head + h], count, stride=R1)
+        at = pl.ds(offset_of(code, 0, h), count, stride=R1)
         first, second = merge((a0[at, :], a1[at, :]), (out[:, :128], out[:, 128:]), peak, h)
         if h < 3:
             a0[at, :] = first
@@ -204,7 +202,7 @@
     first = jnp.zeros((wide, 128), F32)
     second = jnp.zeros((wide, 128), F32)
     for h in range(4):
-        at = pl.ds(offsets[1, first_head + h], wide, stride=R2)
+        at = pl.ds(offset_of(code, 1, h), wide, stride=R2)
         here0, here1 = a0[at, :], a1[at, :]
         first = jnp.where(head_tile_all(h, 0), here0, first)
         second = jnp.where(head_tile_all(h, 1), here1, second)
@@ -233,7 +231,7 @@
     return [(lax.rem(chip + step + n_chips, n_chips), core) for step, core in pieces]
 
 
-def wide_kernel(tok_rows, n_chips, plan, last, offsets, valid, qw_ref, accw_ref, *refs):
+def wide_kernel(tok_rows, n_chips, plan, last, code, valid, qw_ref, accw_ref, *refs):
     keys, (out_ref, ka, va) = refs[: len(plan)], refs[len(plan) :]
     core = lax.rem(lax.axis_index("seq"), 2)
     count = qw_ref.shape[0] // 4
@@ -242,7 +240,7 @@
         for i, (chip, core_of) in enumerate(gathered_from(n_chips, 1 - core if swapped else core, group)):
             at = slice(base, base + count)
             first = (chip * 2 + core_of) * tok_rows
-            open_piece(ref[i * count : (i + 1) * count], first, R2, offsets, 1, valid, ka, va, at)
+            open_piece(ref[i * count : (i + 1) * count], first, R2, code, 1, valid, ka, va, at)
             base += count
     peak, out = attend(qw_ref[...], ka[...], va[...])
     first, second = accw_ref[0], accw_ref[1]
@@ -266,9 +264,11 @@
     return [lax.rem(sub + step + subs, subs) for step in X_FROM]
 
 
-def final_kernel(offsets, valid, w_ref, a0_ref, a1_ref, a2_ref, a3_ref, b0_ref, b1_ref, b2_ref, b3_ref,
-                 out_ref, f0, f1, wp):
+def final_kernel(offs_hbm, valid, w_ref, a0_ref, a1_ref, a2_ref, a3_ref, b0_ref, b1_ref, b2_ref, b3_ref,
+                 out_ref, f0, f1, wp, offsets, sem):
     cols, rows = out_ref.shape
+    fetch = pltpu.make_async_copy(offs_hbm, offsets, sem)
+    fetch.start()
     half, count, chunk = rows // 2, rows // R2, 256
     sources = x_sources()
     wp[...] = jnp.zeros(wp.shape, BF16)
@@ -290,6 +290,7 @@
             total = jnp.dot(x, wp[part], preferred_element_type=F32)
             f0[at, :] = total[:, :128]
             f1[at, :] = total[:, 128:]
+    fetch.wait()
     for i, ref in enumerate((b0_ref, b1_ref, b2_ref, b3_ref)):
         tail = ref[count:].astype(F32)
         second = jnp.concatenate([tail, pltpu.roll(tail, 64, 1)], axis=0)
@@ -331,6 +332,9 @@
     n_sub = lax.axis_size("sub")
     n_chips = n_seq // 2
     mid, wide = rows // R1, rows // R2
+    shifts = 6 * lax.broadcasted_iota(jnp.int32, (2, 4), 1) + 2 * lax.broadcasted_iota(jnp.int32, (2, 4), 0)
+    mine = lax.dynamic_slice_in_dim(offsets, sub * 4, 4, 1)
+    code = (jnp.sum(jnp.left_shift(mine, shifts)) | (sub << 24)).reshape(1)
     w_cols = lax.dynamic_slice_in_dim(w_out, sub * cols, cols, 1)
 
     def along_z(value, up, down):
@@ -345,6 +349,7 @@
 
     smem_offsets = pltpu.SMEM(offsets.shape, jnp.int32)
     q_t, k_t, v_t = q_heads.T, k_heads.T, v_heads.T
+    near_q, w_cols = lax.optimization_barrier((q_t, w_cols))
     kv_mid, kv_wide = call(
         prep_kernel, "aaa",
         [((mid, 384), BF16), ((wide, 384), BF16)],
@@ -358,12 +363,11 @@
     own_pair = jnp.concatenate([kv_wide, kv_both], axis=0)
     far4 = along_z(own_pair, four, -four)
     acc, q_mid, q_wide = call(
-        near_kernel, "savvv",
+        near_kernel, "ssvvv",
         [((2, rows, 128), F32), ((4 * mid, 256), BF16), ((4 * wide, 256), BF16)],
-        [((rows, 256), BF16), ((256, rows), BF16), ((256, rows), BF16)] + [((rows, 128), F32)] * 2
-        + [smem_offsets, pltpu.SemaphoreType.DMA],
+        [((rows, 256), BF16), ((256, rows), BF16), ((256, rows), BF16)] + [((rows, 128), F32)] * 2,
         4e9, 28,
-    )(valid, offsets, q_t, k_t, v_t)
+    )(code, valid, near_q, k_t, v_t)
     far_mid, acc = lax.optimization_barrier((far_mid, acc))
 
     swap_mid = flipped(jnp.concatenate([kv_mid, far_mid], axis=0), 1)
@@ -377,7 +381,7 @@
         [((rows + rows // 2, 128), BF16), ((2, wide, 128), F32)],
         [((4 * mid, 256), BF16)] * 2 + [((rows, 128), F32)] * 2,
         1e9,
-    )(offsets, valid, acc, q_mid, kv_mid, far_mid, swap_mid)
+    )(code, valid, acc, q_mid, kv_mid, far_mid, swap_mid)
     attns = [along_x(attn, s) for s in (1, n_sub - 1, 2)]
 
     def wide_part(plan, acc_now, keys, last=False):
@@ -386,7 +390,7 @@
             functools.partial(wide_kernel, rows, n_chips, plan, last), "ssvv" + "v" * len(keys),
             [((wide + wide // 2, 128), BF16) if last else ((2, wide, 128), F32)],
             [((n_keys, 256), BF16)] * 2, 5e8,
-        )(offsets, valid, q_wide, acc_now, *keys)
+        )(code, valid, q_wide, acc_now, *keys)
         return result
 
     early = jnp.concatenate([mine, around2], axis=0)
@@ -398,8 +402,9 @@
     attn_wide = wide_part(((1, True),), acc_wide, (late_other,), last=True)
     wides = [along_x(attn_wide, s) for s in (1, n_sub - 1, 2)]
     (out,) = call(
-        final_kernel, "ssv" + "v" * 8, [((cols, rows), BF16)],
-        [((rows, 128), F32)] * 2 + [((2, 4 * 256, 256), BF16)], 1e9,
+        final_kernel, "asv" + "v" * 8, [((cols, rows), BF16)],
+        [((rows, 128), F32)] * 2
+        + [((2, 4 * 256, 256), BF16), smem_offsets, pltpu.SemaphoreType.DMA], 1e9,
     )(offsets, valid, w_cols, attn, *attns, attn_wide, *wides)
     return out.T
 

time: 94.8 us -> 91.3 us (0.963)
  the two profiles are of different devices: /device:TPU:40 before, /device:TPU:33 now
where the time goes in v1:
time: 91.3 us; the launch traced here: 90.1 us
  starting transfers between devices  51.9 us (57%)
  Pallas kernels  17.7 us (19%)
  waiting for transfers between devices  17.7 us (19%)
  between operations  1.67 us (2%)
    ppermute x5, starting transfers between devices, flipped(): return lax.ppermute(value, 'seq', [(i, i ^ mask) for i in range(n_seq)])  26.6 us
    ppermute x5, starting transfers between devices, along_z(): return lax.ppermute(value, 'seq', pairs)  14.4 us
    ppermute x6, starting transfers between devices, along_x(): lax.ppermute(value, 'sub', [(i, (i + step) % n_sub) for i in range(n_sub)])  11 us
    ppermute x6, waiting for transfers between devices, along_x(): lax.ppermute(value, 'sub', [(i, (i + step) % n_sub) for i in range(n_sub)])  9.6 us
    ppermute x5, waiting for transfers between devices, along_z(): return lax.ppermute(value, 'seq', pairs)  8.06 us
    pallas_call x1, Pallas kernels, local(): call(near_kernel, 'ssvvv', [((2, rows, 128), F32), ((4 * mid, 256), BF16)...  6.18 us
    pallas_call x3, Pallas kernels, wide_part(): call(functools.partial(wide_kernel, rows, n_chips, plan, last), 'ssvv' +...  3.16 us
    pallas_call x1, Pallas kernels, local(): call(functools.partial(middle_kernel, rows), 'ssvvvvv', [((rows + rows //...  3.05 us
  transfers between devices with their start and end apart: 16, of which 5 were waited for; matrix products, arithmetic and copies ran while one was open for 1% of the time, Pallas kernels for 14%

profile of v1, /device:TPU:33, one launch (start us, length us, event | category | flops | bytes accessed | tf_op | source)
XLA Modules:
  0.0 90.1 jit_solution(10440167650230784294)
XLA Ops:
  0.0 0.0 copy-start
  0.0 0.0 copy-start.4
  0.0 0.0 copy-start.1
  0.0 0.0 copy-start.2
  0.0 0.0 copy-start.5
  0.0 2.5 %shard_map.64 = (bf16[256,384]{1,0:T(8,128)(2,1)}, bf16[64,384]{1,0:T(8,128)(2,1)}) custom-call(s32[2,16]{1,0:T(2,128)} %offs_hbm.3, bf16[192,1024]{1,0:T(8,128)(2,1)} %bitcast.5, bf16[192,1024]{1,0:T(8,128)(2,1)} %bitcast.7), custom_call_target="tpu_custom_call" | custom-call | flops 200000000 | bytes 2097152 | tf_op jit(solution)/shard_map/pallas_call | solution.py:353
  2.5 3.4 %collective-permute-start = (bf16[256,384]{1,0:T(8,128)(2,1)}, bf16[256,384]{1,0:T(8,128)(2,1)S(1)}, u32[]{:S(2)}, u32[]{:S(2)}) collective-permute-start(bf16[256,384]{1,0:T(8,128)(2,1)} %get-tuple-element.17.own_ref), channel_id=1, source_target_pairs={{0,8},{4,12},{8,0},{12,4},{16,24},{20,28},{24,16},{28,20},{32,40},... | collective-permute-start | bytes 589832 | tf_op jit(solution)/shard_map/ppermute | solution.py:345
  6.0 17.2 %collective-permute-start.5 = (bf16[64,384]{1,0:T(8,128)(2,1)}, bf16[64,384]{1,0:T(8,128)(2,1)S(1)}, u32[]{:S(2)}, u32[]{:S(2)}) collective-permute-start(bf16[64,384]{1,0:T(8,128)(2,1)} %get-tuple-element.26), channel_id=1, source_target_pairs={{0,4},{4,0},{8,12},{12,8},{16,20},{20,16},{24,28},{28,24},{32,36},... | collective-permute-start | bytes 147464 | tf_op jit(solution)/shard_map/ppermute | solution.py:345
  23.9 0.0 copy-done
  23.9 0.2 constant_dynamic-slice_fusion.w_ref
  24.1 0.0 copy-done.4
  24.1 0.7 shift-left_reduce_fusion
  25.4 0.0 copy-done.1
  25.4 0.0 copy-done.2
  25.5 0.0 copy-done.5
  25.5 0.0 copy-start.6
  25.5 6.2 %shard_map.65 = (f32[2,1024,128]{2,1,0:T(8,128)S(1)}, bf16[1024,256]{1,0:T(8,128)(2,1)S(1)}, bf16[256,256]{1,0:T(8,128)(2,1)S(1)}) custom-call(s32[1]{0:T(128)} %bitcast.1.code, s32[1]{0:T(128)S(6)} %copy.13.valid, bf16[192,1024]{1,0:T(8,128)(2,1)S(1)} %bitcast.9, bf16[192,1024]{1,0:T(8,128)(2,1)S(1)} %bitcast.6, bf16[192,1024]{1,0:T(8,128)(2,1)S(1)} %bitcast.8), custom_call_target="tpu_custom_call" | custom-call | flops 4000000000 | bytes 2097152 | tf_op jit(solution)/shard_map/pallas_call | solution.py:365
  31.7 0.0 copy-start.3
  31.7 0.0 collective-permute-done.5
  31.7 0.0 copy-done.6
  31.7 3.7 %collective-permute-start.6 = (bf16[128,384]{1,0:T(8,128)(2,1)S(1)}, bf16[128,384]{1,0:T(8,128)(2,1)S(1)}, u32[]{:S(2)}, u32[]{:S(2)}) collective-permute-start(bf16[128,384]{1,0:T(8,128)(2,1)S(1)} %pad_maximum_fusion.2), channel_id=1, source_target_pairs={{0,32},{4,100},{8,40},{12,108},{16,48},{20,116},{24,56},{28,124},{... | collective-permute-start | bytes 294920 | tf_op jit(solution)/shard_map/ppermute | solution.py:342
  35.4 4.1 %collective-permute-done.6 = bf16[128,384]{1,0:T(8,128)(2,1)S(1)} collective-permute-done((bf16[128,384]{1,0:T(8,128)(2,1)S(1)}, bf16[128,384]{1,0:T(8,128)(2,1)S(1)}, u32[]{:S(2)}, u32[]{:S(2)}) %collective-permute-start.6) | collective-permute-done | bytes 98336 | tf_op jit(solution)/shard_map/ppermute | solution.py:342
  39.5 4.2 %collective-permute-start.7 = (bf16[64,384]{1,0:T(8,128)(2,1)S(1)}, bf16[64,384]{1,0:T(8,128)(2,1)S(1)}, u32[]{:S(2)}, u32[]{:S(2)}) collective-permute-start(bf16[64,384]{1,0:T(8,128)(2,1)S(1)} %slice.4), channel_id=1, source_target_pairs={{0,32},{4,100},{8,40},{12,108},{16,48},{20,116},{24,56},{28,124},{... | collective-permute-start | bytes 147464 | tf_op jit(solution)/shard_map/ppermute | solution.py:342
  43.8 2.1 %collective-permute-start.8 = (bf16[256,384]{1,0:T(8,128)(2,1)S(1)}, bf16[256,384]{1,0:T(8,128)(2,1)S(1)}, u32[]{:S(2)}, u32[]{:S(2)}) collective-permute-start(bf16[256,384]{1,0:T(8,128)(2,1)S(1)} %pad_maximum_fusion.1), channel_id=1, source_target_pairs={{0,16},{4,116},{8,24},{12,124},{16,32},{20,4},{24,40},{28,12},{32,... | collective-permute-start | bytes 589832 | tf_op jit(solution)/shard_map/ppermute | solution.py:342
  45.9 0.5 collective-permute-done.7
  46.4 0.0 collective-permute-done.far_ref
  46.4 1.8 %collective-permute-start.10 = (bf16[256,384]{1,0:T(8,128)(2,1)S(1)}, bf16[256,384]{1,0:T(8,128)(2,1)S(1)}, u32[]{:S(2)}, u32[]{:S(2)}) collective-permute-start(bf16[256,384]{1,0:T(8,128)(2,1)S(1)} %get-tuple-element.29), channel_id=1, source_target_pairs={{0,8},{4,12},{8,16},{12,20},{16,24},{20,28},{24,32},{28,36},{32,40... | collective-permute-start | bytes 589832 | tf_op jit(solution)/shard_map/ppermute | solution.py:342
  48.1 0.0 copy-done.3
  48.2 4.0 %collective-permute-start.1 = (bf16[512,384]{1,0:T(8,128)(2,1)S(1)}, bf16[512,384]{1,0:T(8,128)(2,1)S(1)}, u32[]{:S(2)}, u32[]{:S(2)}) collective-permute-start(bf16[512,384]{1,0:T(8,128)(2,1)S(1)} %pad_maximum_fusion), channel_id=1, source_target_pairs={{0,4},{4,0},{8,12},{12,8},{16,20},{20,16},{24,28},{28,24},{32,36},... | collective-permute-start | bytes 1179656 | tf_op jit(solution)/shard_map/ppermute | solution.py:345
  52.2 2.6 %collective-permute-start.11 = (bf16[256,384]{1,0:T(8,128)(2,1)S(1)}, bf16[256,384]{1,0:T(8,128)(2,1)S(1)}, u32[]{:S(2)}, u32[]{:S(2)}) collective-permute-start(bf16[256,384]{1,0:T(8,128)(2,1)S(1)} %get-tuple-element.29), channel_id=1, source_target_pairs={{0,120},{4,124},{8,0},{12,4},{16,8},{20,12},{24,16},{28,20},{32,24... | collective-permute-start | bytes 589832 | tf_op jit(solution)/shard_map/ppermute | solution.py:342
  54.8 0.0 collective-permute-done.8
  54.9 0.5 collective-permute-start.9
  55.4 0.0 collective-permute-done.10
  55.4 3.5 %collective-permute-done.11 = bf16[256,384]{1,0:T(8,128)(2,1)S(1)} collective-permute-done((bf16[256,384]{1,0:T(8,128)(2,1)S(1)}, bf16[256,384]{1,0:T(8,128)(2,1)S(1)}, u32[]{:S(2)}, u32[]{:S(2)}) %collective-permute-start.11) | collective-permute-done | bytes 196640 | tf_op jit(solution)/shard_map/ppermute | solution.py:342
  59.0 1.3 %collective-permute-start.12 = (bf16[512,384]{1,0:T(8,128)(2,1)S(1)}, bf16[512,384]{1,0:T(8,128)(2,1)S(1)}, u32[]{:S(2)}, u32[]{:S(2)}) collective-permute-start(bf16[512,384]{1,0:T(8,128)(2,1)S(1)} %constant_dynamic-update-slice_fusion.7.refs_0_), channel_id=1, source_target_pairs={{0,4},{4,0},{8,12},{12,8},{16,20},{20,16},{24,28},{28,24},{32,36},... | collective-permute-start | bytes 1179656 | tf_op jit(solution)/shard_map/ppermute | solution.py:345
  60.3 0.0 collective-permute-done.1.swap_ref
  60.3 3.1 %shard_map.66 = (bf16[1536,128]{1,0:T(8,128)(2,1)S(1)}, f32[2,64,128]{2,1,0:T(8,128)S(1)}) custom-call(s32[1]{0:T(128)} %bitcast.1.code, s32[1]{0:T(128)S(6)} %copy.13.valid, f32[2,1024,128]{2,1,0:T(8,128)S(1)} %get-tuple-element.20.acc_ref, bf16[1024,256]{1,0:T(8,128)(2,1)S(1)} %get-tuple-element.21.qm_ref, bf16[256,384]{1,0:T(8,128)(2,1)S(1)} %copy-done.3, ...), custom_call_target="tpu_custom_call" | custom-call | flops 1000000000 | bytes 2097152 | tf_op jit(solution)/shard_map/pallas_call | solution.py:379
  63.3 1.7 %collective-permute-start.2 = (bf16[1536,128]{1,0:T(8,128)(2,1)S(1)}, bf16[1536,128]{1,0:T(8,128)(2,1)S(1)}, u32[]{:S(2)}, u32[]{:S(2)}) collective-permute-start(bf16[1536,128]{1,0:T(8,128)(2,1)S(1)} %get-tuple-element.23.a0_ref), channel_id=1, source_target_pairs={{0,1},{1,2},{2,3},{3,0},{4,5},{5,6},{6,7},{7,4},{8,9},{9,10},{10,1... | collective-permute-start | bytes 1179656 | tf_op jit(solution)/shard_map/ppermute | solution.py:348
  65.0 1.7 %collective-permute-start.3 = (bf16[1536,128]{1,0:T(8,128)(2,1)S(1)}, bf16[1536,128]{1,0:T(8,128)(2,1)S(1)}, u32[]{:S(2)}, u32[]{:S(2)}) collective-permute-start(bf16[1536,128]{1,0:T(8,128)(2,1)S(1)} %get-tuple-element.23.a0_ref), channel_id=1, source_target_pairs={{0,3},{1,0},{2,1},{3,2},{4,7},{5,4},{6,5},{7,6},{8,11},{9,8},{10,9... | collective-permute-start | bytes 1179656 | tf_op jit(solution)/shard_map/ppermute | solution.py:348
  66.7 1.4 %collective-permute-start.4 = (bf16[1536,128]{1,0:T(8,128)(2,1)S(1)}, bf16[1536,128]{1,0:T(8,128)(2,1)S(1)}, u32[]{:S(2)}, u32[]{:S(2)}) collective-permute-start(bf16[1536,128]{1,0:T(8,128)(2,1)S(1)} %get-tuple-element.23.a0_ref), channel_id=1, source_target_pairs={{0,2},{1,3},{2,0},{3,1},{4,6},{5,7},{6,4},{7,5},{8,10},{9,11},{10,... | collective-permute-start | bytes 1179656 | tf_op jit(solution)/shard_map/ppermute | solution.py:348
  68.1 0.0 collective-permute-done.9.refs_1_
  68.1 1.2 %shard_map.67.accw_ref = f32[2,64,128]{2,1,0:T(8,128)S(1)} custom-call(s32[1]{0:T(128)} %bitcast.1.code, s32[1]{0:T(128)S(6)} %copy.13.valid, bf16[256,256]{1,0:T(8,128)(2,1)S(1)} %get-tuple-element.24.qw_ref, f32[2,64,128]{2,1,0:T(8,128)S(1)} %get-tuple-element.25.accw_ref, bf16[512,384]{1,0:T(8,128)(2,1)S(1)} %constant_dynamic-update-slice_fusion.refs_0_, ...), custom_call_target="tpu_custom_call" | custom-call | flops 500000000 | bytes 2097152 | tf_op jit(solution)/shard_map/pallas_call | solution.py:389
  69.3 0.9 %shard_map.68.accw_ref = f32[2,64,128]{2,1,0:T(8,128)S(1)} custom-call(s32[1]{0:T(128)} %bitcast.1.code, s32[1]{0:T(128)S(6)} %copy.13.valid, bf16[256,256]{1,0:T(8,128)(2,1)S(1)} %get-tuple-element.24.qw_ref, f32[2,64,128]{2,1,0:T(8,128)S(1)} %shard_map.67.accw_ref, bf16[512,384]{1,0:T(8,128)(2,1)S(1)} %constant_dynamic-update-slice_fusion.7.refs_0_), custom_call_target="tpu_custom_call" | custom-call | flops 500000000 | bytes 2097152 | tf_op jit(solution)/shard_map/pallas_call | solution.py:389
  70.2 0.0 collective-permute-done.12.refs_0_
  70.3 1.1 %shard_map.69.b0_ref = bf16[96,128]{1,0:T(8,128)(2,1)S(1)} custom-call(s32[1]{0:T(128)} %bitcast.1.code, s32[1]{0:T(128)S(6)} %copy.13.valid, bf16[256,256]{1,0:T(8,128)(2,1)S(1)} %get-tuple-element.24.qw_ref, f32[2,64,128]{2,1,0:T(8,128)S(1)} %shard_map.68.accw_ref, bf16[512,384]{1,0:T(8,128)(2,1)S(1)} %collective-permute-done.12.refs_0_), custom_call_target="tpu_custom_call" | custom-call | flops 500000000 | bytes 2097152 | tf_op jit(solution)/shard_map/pallas_call | solution.py:389
  71.3 0.5 collective-permute-start.13
  71.9 2.2 %collective-permute-start.14 = (bf16[96,128]{1,0:T(8,128)(2,1)S(1)}, bf16[96,128]{1,0:T(8,128)(2,1)S(1)}, u32[]{:S(2)}, u32[]{:S(2)}) collective-permute-start(bf16[96,128]{1,0:T(8,128)(2,1)S(1)} %shard_map.69.b0_ref), channel_id=1, source_target_pairs={{0,3},{1,0},{2,1},{3,2},{4,7},{5,4},{6,5},{7,6},{8,11},{9,8},{10,9... | collective-permute-start | bytes 73736 | tf_op jit(solution)/shard_map/ppermute | solution.py:348
  74.1 8.4 %collective-permute-done.13.b1_ref = bf16[96,128]{1,0:T(8,128)(2,1)S(1)} collective-permute-done((bf16[96,128]{1,0:T(8,128)(2,1)S(1)}, bf16[96,128]{1,0:T(8,128)(2,1)S(1)}, u32[]{:S(2)}, u32[]{:S(2)}) %collective-permute-start.13) | collective-permute-done | bytes 24608 | tf_op jit(solution)/shard_map/ppermute | solution.py:348
  82.5 3.4 %collective-permute-start.15 = (bf16[96,128]{1,0:T(8,128)(2,1)S(1)}, bf16[96,128]{1,0:T(8,128)(2,1)S(1)}, u32[]{:S(2)}, u32[]{:S(2)}) collective-permute-start(bf16[96,128]{1,0:T(8,128)(2,1)S(1)} %shard_map.69.b0_ref), channel_id=1, source_target_pairs={{0,2},{1,3},{2,0},{3,1},{4,6},{5,7},{6,4},{7,5},{8,10},{9,11},{10,... | collective-permute-start | bytes 73736 | tf_op jit(solution)/shard_map/ppermute | solution.py:348
  85.9 0.0 collective-permute-done.14.b2_ref
  85.9 1.2 %collective-permute-done.15.b3_ref = bf16[96,128]{1,0:T(8,128)(2,1)S(1)} collective-permute-done((bf16[96,128]{1,0:T(8,128)(2,1)S(1)}, bf16[96,128]{1,0:T(8,128)(2,1)S(1)}, u32[]{:S(2)}, u32[]{:S(2)}) %collective-permute-start.15) | collective-permute-done | bytes 24608 | tf_op jit(solution)/shard_map/ppermute | solution.py:348
  87.1 0.0 collective-permute-done.2.a1_ref
  87.1 0.0 collective-permute-done.3.a2_ref
  87.1 0.0 collective-permute-done.4.a3_ref
  87.1 2.9 %shard_map.70 = bf16[192,1024]{1,0:T(8,128)(2,1)} custom-call(s32[2,16]{1,0:T(2,128)S(1)} %copy-done.4, s32[1]{0:T(128)S(6)} %copy.13.valid, bf16[768,192]{1,0:T(8,128)(2,1)S(1)} %constant_dynamic-slice_fusion.w_ref, bf16[1536,128]{1,0:T(8,128)(2,1)S(1)} %get-tuple-element.23.a0_ref, bf16[1536,128]{1,0:T(8,128)(2,1)S(1)} %collective-permute-done.2.a1_ref, ...), custom_call_target="tpu_custom_call" | custom-call | flops 1000000000 | bytes 2097152 | tf_op jit(solution)/shard_map/pallas_call | solution.py:404
  (12 shorter events, 0.2 us)
Async XLA Ops:
  0.0 23.9 %copy-start = (bf16[768,768]{1,0:T(8,128)(2,1)S(1)}, bf16[768,768]{1,0:T(8,128)(2,1)}, u32[]{:S(2)}) copy-start(bf16[768,768]{1,0:T(8,128)(2,1)} %param.9) | copy-start | bytes 3538948
  0.0 24.1 %copy-start.4 = (s32[2,16]{1,0:T(2,128)S(1)}, s32[2,16]{1,0:T(2,128)}, u32[]{:S(2)}) copy-start(s32[2,16]{1,0:T(2,128)} %offs_hbm.3) | copy-start | bytes 388
  0.0 25.4 %copy-start.1 = (bf16[1024,192]{0,1:T(8,128)(2,1)S(1)}, bf16[1024,192]{0,1:T(8,128)(2,1)}, u32[]{:S(2)}) copy-start(bf16[1024,192]{0,1:T(8,128)(2,1)} %param.7) | copy-start | bytes 1179652
  0.0 25.4 %copy-start.2 = (bf16[1024,192]{0,1:T(8,128)(2,1)S(1)}, bf16[1024,192]{0,1:T(8,128)(2,1)}, u32[]{:S(2)}) copy-start(bf16[1024,192]{0,1:T(8,128)(2,1)} %param.8) | copy-start | bytes 1179652
  0.0 25.4 %copy-start.5 = (bf16[1024,192]{0,1:T(8,128)(2,1)S(1)}, bf16[1024,192]{0,1:T(8,128)(2,1)}, u32[]{:S(2)}) copy-start(bf16[1024,192]{0,1:T(8,128)(2,1)} %param.6) | copy-start | bytes 1179652
  2.5 43.9 %collective-permute-start = (bf16[256,384]{1,0:T(8,128)(2,1)}, bf16[256,384]{1,0:T(8,128)(2,1)S(1)}, u32[]{:S(2)}, u32[]{:S(2)}) collective-permute-start(bf16[256,384]{1,0:T(8,128)(2,1)} %get-tuple-element.17.own_ref), channel_id=1, source_target_pairs={{0,8},{4,12},{8,0},{12,4},{16,24},{20,28},{24,16},{28,20},{32,40},... | collective-permute-start | bytes 589832 | tf_op jit(solution)/shard_map/ppermute | solution.py:345
  6.0 25.7 %collective-permute-start.5 = (bf16[64,384]{1,0:T(8,128)(2,1)}, bf16[64,384]{1,0:T(8,128)(2,1)S(1)}, u32[]{:S(2)}, u32[]{:S(2)}) collective-permute-start(bf16[64,384]{1,0:T(8,128)(2,1)} %get-tuple-element.26), channel_id=1, source_target_pairs={{0,4},{4,0},{8,12},{12,8},{16,20},{20,16},{24,28},{28,24},{32,36},... | collective-permute-start | bytes 147464 | tf_op jit(solution)/shard_map/ppermute | solution.py:345
  25.5 6.2 %copy-start.6 = (bf16[64,384]{1,0:T(8,128)(2,1)S(1)}, bf16[64,384]{1,0:T(8,128)(2,1)}, u32[]{:S(2)}) copy-start(bf16[64,384]{1,0:T(8,128)(2,1)} %get-tuple-element.26) | copy-start | bytes 147460
  31.7 16.5 %copy-start.3 = (bf16[256,384]{1,0:T(8,128)(2,1)S(1)}, bf16[256,384]{1,0:T(8,128)(2,1)}, u32[]{:S(2)}) copy-start(bf16[256,384]{1,0:T(8,128)(2,1)} %get-tuple-element.17.own_ref) | copy-start | bytes 589828
  31.7 7.8 %collective-permute-start.6 = (bf16[128,384]{1,0:T(8,128)(2,1)S(1)}, bf16[128,384]{1,0:T(8,128)(2,1)S(1)}, u32[]{:S(2)}, u32[]{:S(2)}) collective-permute-start(bf16[128,384]{1,0:T(8,128)(2,1)S(1)} %pad_maximum_fusion.2), channel_id=1, source_target_pairs={{0,32},{4,100},{8,40},{12,108},{16,48},{20,116},{24,56},{28,124},{... | collective-permute-start | bytes 294920 | tf_op jit(solution)/shard_map/ppermute | solution.py:342
  39.5 6.8 %collective-permute-start.7 = (bf16[64,384]{1,0:T(8,128)(2,1)S(1)}, bf16[64,384]{1,0:T(8,128)(2,1)S(1)}, u32[]{:S(2)}, u32[]{:S(2)}) collective-permute-start(bf16[64,384]{1,0:T(8,128)(2,1)S(1)} %slice.4), channel_id=1, source_target_pairs={{0,32},{4,100},{8,40},{12,108},{16,48},{20,116},{24,56},{28,124},{... | collective-permute-start | bytes 147464 | tf_op jit(solution)/shard_map/ppermute | solution.py:342
  43.8 11.1 %collective-permute-start.8 = (bf16[256,384]{1,0:T(8,128)(2,1)S(1)}, bf16[256,384]{1,0:T(8,128)(2,1)S(1)}, u32[]{:S(2)}, u32[]{:S(2)}) collective-permute-start(bf16[256,384]{1,0:T(8,128)(2,1)S(1)} %pad_maximum_fusion.1), channel_id=1, source_target_pairs={{0,16},{4,116},{8,24},{12,124},{16,32},{20,4},{24,40},{28,12},{32,... | collective-permute-start | bytes 589832 | tf_op jit(solution)/shard_map/ppermute | solution.py:342
  46.4 9.0 %collective-permute-start.10 = (bf16[256,384]{1,0:T(8,128)(2,1)S(1)}, bf16[256,384]{1,0:T(8,128)(2,1)S(1)}, u32[]{:S(2)}, u32[]{:S(2)}) collective-permute-start(bf16[256,384]{1,0:T(8,128)(2,1)S(1)} %get-tuple-element.29), channel_id=1, source_target_pairs={{0,8},{4,12},{8,16},{12,20},{16,24},{20,28},{24,32},{28,36},{32,40... | collective-permute-start | bytes 589832 | tf_op jit(solution)/shard_map/ppermute | solution.py:342
  48.2 12.1 %collective-permute-start.1 = (bf16[512,384]{1,0:T(8,128)(2,1)S(1)}, bf16[512,384]{1,0:T(8,128)(2,1)S(1)}, u32[]{:S(2)}, u32[]{:S(2)}) collective-permute-start(bf16[512,384]{1,0:T(8,128)(2,1)S(1)} %pad_maximum_fusion), channel_id=1, source_target_pairs={{0,4},{4,0},{8,12},{12,8},{16,20},{20,16},{24,28},{28,24},{32,36},... | collective-permute-start | bytes 1179656 | tf_op jit(solution)/shard_map/ppermute | solution.py:345
  52.2 6.7 %collective-permute-start.11 = (bf16[256,384]{1,0:T(8,128)(2,1)S(1)}, bf16[256,384]{1,0:T(8,128)(2,1)S(1)}, u32[]{:S(2)}, u32[]{:S(2)}) collective-permute-start(bf16[256,384]{1,0:T(8,128)(2,1)S(1)} %get-tuple-element.29), channel_id=1, source_target_pairs={{0,120},{4,124},{8,0},{12,4},{16,8},{20,12},{24,16},{28,20},{32,24... | collective-permute-start | bytes 589832 | tf_op jit(solution)/shard_map/ppermute | solution.py:342
  54.9 13.3 %collective-permute-start.9 = (bf16[512,384]{1,0:T(8,128)(2,1)S(1)}, bf16[512,384]{1,0:T(8,128)(2,1)S(1)}, u32[]{:S(2)}, u32[]{:S(2)}) collective-permute-start(bf16[512,384]{1,0:T(8,128)(2,1)S(1)} %constant_dynamic-update-slice_fusion.refs_0_), channel_id=1, source_target_pairs={{0,4},{4,0},{8,12},{12,8},{16,20},{20,16},{24,28},{28,24},{32,36},... | collective-permute-start | bytes 1179656 | tf_op jit(solution)/shard_map/ppermute | solution.py:345
  59.0 11.3 %collective-permute-start.12 = (bf16[512,384]{1,0:T(8,128)(2,1)S(1)}, bf16[512,384]{1,0:T(8,128)(2,1)S(1)}, u32[]{:S(2)}, u32[]{:S(2)}) collective-permute-start(bf16[512,384]{1,0:T(8,128)(2,1)S(1)} %constant_dynamic-update-slice_fusion.7.refs_0_), channel_id=1, source_target_pairs={{0,4},{4,0},{8,12},{12,8},{16,20},{20,16},{24,28},{28,24},{32,36},... | collective-permute-start | bytes 1179656 | tf_op jit(solution)/shard_map/ppermute | solution.py:345
  63.3 23.7 %collective-permute-start.2 = (bf16[1536,128]{1,0:T(8,128)(2,1)S(1)}, bf16[1536,128]{1,0:T(8,128)(2,1)S(1)}, u32[]{:S(2)}, u32[]{:S(2)}) collective-permute-start(bf16[1536,128]{1,0:T(8,128)(2,1)S(1)} %get-tuple-element.23.a0_ref), channel_id=1, source_target_pairs={{0,1},{1,2},{2,3},{3,0},{4,5},{5,6},{6,7},{7,4},{8,9},{9,10},{10,1... | collective-permute-start | bytes 1179656 | tf_op jit(solution)/shard_map/ppermute | solution.py:348
  65.0 22.1 %collective-permute-start.3 = (bf16[1536,128]{1,0:T(8,128)(2,1)S(1)}, bf16[1536,128]{1,0:T(8,128)(2,1)S(1)}, u32[]{:S(2)}, u32[]{:S(2)}) collective-permute-start(bf16[1536,128]{1,0:T(8,128)(2,1)S(1)} %get-tuple-element.23.a0_ref), channel_id=1, source_target_pairs={{0,3},{1,0},{2,1},{3,2},{4,7},{5,4},{6,5},{7,6},{8,11},{9,8},{10,9... | collective-permute-start | bytes 1179656 | tf_op jit(solution)/shard_map/ppermute | solution.py:348
  66.7 20.4 %collective-permute-start.4 = (bf16[1536,128]{1,0:T(8,128)(2,1)S(1)}, bf16[1536,128]{1,0:T(8,128)(2,1)S(1)}, u32[]{:S(2)}, u32[]{:S(2)}) collective-permute-start(bf16[1536,128]{1,0:T(8,128)(2,1)S(1)} %get-tuple-element.23.a0_ref), channel_id=1, source_target_pairs={{0,2},{1,3},{2,0},{3,1},{4,6},{5,7},{6,4},{7,5},{8,10},{9,11},{10,... | collective-permute-start | bytes 1179656 | tf_op jit(solution)/shard_map/ppermute | solution.py:348
  71.3 11.1 %collective-permute-start.13 = (bf16[96,128]{1,0:T(8,128)(2,1)S(1)}, bf16[96,128]{1,0:T(8,128)(2,1)S(1)}, u32[]{:S(2)}, u32[]{:S(2)}) collective-permute-start(bf16[96,128]{1,0:T(8,128)(2,1)S(1)} %shard_map.69.b0_ref), channel_id=1, source_target_pairs={{0,1},{1,2},{2,3},{3,0},{4,5},{5,6},{6,7},{7,4},{8,9},{9,10},{10,1... | collective-permute-start | bytes 73736 | tf_op jit(solution)/shard_map/ppermute | solution.py:348
  71.9 14.0 %collective-permute-start.14 = (bf16[96,128]{1,0:T(8,128)(2,1)S(1)}, bf16[96,128]{1,0:T(8,128)(2,1)S(1)}, u32[]{:S(2)}, u32[]{:S(2)}) collective-permute-start(bf16[96,128]{1,0:T(8,128)(2,1)S(1)} %shard_map.69.b0_ref), channel_id=1, source_target_pairs={{0,3},{1,0},{2,1},{3,2},{4,7},{5,4},{6,5},{7,6},{8,11},{9,8},{10,9... | collective-permute-start | bytes 73736 | tf_op jit(solution)/shard_map/ppermute | solution.py:348
  82.5 4.6 %collective-permute-start.15 = (bf16[96,128]{1,0:T(8,128)(2,1)S(1)}, bf16[96,128]{1,0:T(8,128)(2,1)S(1)}, u32[]{:S(2)}, u32[]{:S(2)}) collective-permute-start(bf16[96,128]{1,0:T(8,128)(2,1)S(1)} %shard_map.69.b0_ref), channel_id=1, source_target_pairs={{0,2},{1,3},{2,0},{3,1},{4,6},{5,7},{6,4},{7,5},{8,10},{9,11},{10,... | collective-permute-start | bytes 73736 | tf_op jit(solution)/shard_map/ppermute | solution.py:348

commit v2 on v1

--- a/solution.py
+++ b/solution.py
@@ -56,7 +56,7 @@
     return peak * LOG2_SCALE, out
 
 
-def prep_kernel(offs_hbm, k_hbm, v_hbm, mid_ref, wide_ref, k_ref, v_ref, offsets, kf, vf, tf, sems):
+def prep_kernel(offs_hbm, k_hbm, v_hbm, mid_ref, wide_ref, code_ref, k_ref, v_ref, offsets, kf, vf, tf, sems):
     copies = [
         pltpu.make_async_copy(source, target, sems.at[i])
         for i, (source, target) in enumerate(
@@ -72,6 +72,9 @@
     vf[...] = v_ref[:128, :].astype(F32).T
     tf[...] = jnp.concatenate([k_ref[128:192, :], v_ref[128:192, :]], axis=0).astype(F32).T
     copies[0].wait()
+    code_ref[0] = sum(
+        offsets[row, first_head + h] << (6 * h + 2 * row) for row in range(2) for h in range(4)
+    )
     lane = lanes()
     for row, stride, out in ((0, R1, mid_ref), (1, R2, wide_ref)):
         count = out.shape[0]
@@ -86,8 +89,11 @@
         out[:, 256:384] = joined.astype(BF16)
 
 
-def near_kernel(code, valid, q_ref, k_ref, v_ref, acc_ref, qm_ref, qw_ref, qa, ka, va, q0, q1):
+def near_kernel(offs_hbm, valid, q_ref, k_ref, v_ref, acc_ref, qm_ref, qw_ref, rows_ref, qa, ka, va, q0, q1, offsets, sem):
     rows = q_ref.shape[1]
+    fetch = pltpu.make_async_copy(offs_hbm, offsets, sem)
+    fetch.start()
+    first_head = lax.axis_index("sub") * 4
     start = lax.axis_index("seq") * rows
     line = lax.broadcasted_iota(jnp.int32, (64, 1), 0)
     ones = jnp.broadcast_to(jnp.where(line < 4, 1.0, 0.0), (64, rows))
@@ -101,14 +107,6 @@
     ka[192:256, :] = jnp.where(line < 4, dead, 0.0).astype(BF16)
     va[:192, :] = v_ref[...]
     va[192:256, :] = ones.astype(BF16)
-
-    for row, stride, out in ((0, R1, qm_ref), (1, R2, qw_ref)):
-        count = rows // stride
-        for h in range(4):
-            for tile, ref in ((0, q0), (1, q1)):
-                picked = ref[pl.ds(offset_of(code, row, h), count, stride=stride), :]
-                picked = jnp.where(head_tile(h, tile), picked, 0.0)
-                out[h * count : (h + 1) * count, tile * 128 : (tile + 1) * 128] = picked.astype(BF16)
 
     chunk = 512
 
@@ -137,6 +135,33 @@
 
     lax.fori_loop(0, rows // chunk, step, 0)
 
+    fetch.wait()
+    for row, stride, out in ((0, R1, qm_ref), (1, R2, qw_ref)):
+        count = rows // stride
+        for h in range(4):
+            for tile, ref in ((0, q0), (1, q1)):
+                picked = ref[pl.ds(offsets[row, first_head + h], count, stride=stride), :]
+                picked = jnp.where(head_tile(h, tile), picked, 0.0)
+                out[h * count : (h + 1) * count, tile * 128 : (tile + 1) * 128] = picked.astype(BF16)
+
+    lane = lanes()
+    one, two = normalised(acc_ref[0], acc_ref[1])
+    line = lax.broadcasted_iota(jnp.int32, (rows, 1), 0)
+    gone0, gone1 = False, False
+    for row, stride in ((0, R1), (1, R2)):
+        by0, by1 = head_vectors([offsets[row, first_head + h] for h in range(4)])
+        gone0 = gone0 | ((line & (stride - 1)) == by0)
+        gone1 = gone1 | ((line & (stride - 1)) == by1)
+    head, tail = packed(jnp.where(gone0, 0.0, one), jnp.where(gone1, 0.0, two))
+    rows_ref[: head.shape[0]] = head
+    rows_ref[head.shape[0] :] = tail
+
+
+def head_vectors(values):
+    lane = lanes()
+    first = jnp.where(lane < HS, values[0], jnp.where(lane < 2 * HS, values[1], values[2]))
+    return first, jnp.where(lane < 16, values[2], values[3])
+
 
 def open_piece(piece, first, stride, code, row, valid, ka, va, at):
     count = piece.shape[0]
@@ -191,10 +216,14 @@
         open_piece(piece, source * tok_rows, R1, code, 0, valid, ka, va, slice(i * count, (i + 1) * count))
     a0[...] = acc_ref[0]
     a1[...] = acc_ref[1]
+    both0 = jnp.zeros((count, 128), F32)
+    both1 = jnp.zeros((count, 128), F32)
     for h in range(4):
         peak, out = attend(qm_ref[h * count : (h + 1) * count], ka[...], va[...])
         at = pl.ds(offset_of(code, 0, h), count, stride=R1)
         first, second = merge((a0[at, :], a1[at, :]), (out[:, :128], out[:, 128:]), peak, h)
+        both0 = jnp.where(head_tile_all(h, 0), first, both0)
+        both1 = jnp.where(head_tile_all(h, 1), second, both1)
         if h < 3:
             a0[at, :] = first
         a1[at, :] = second
@@ -203,17 +232,17 @@
     second = jnp.zeros((wide, 128), F32)
     for h in range(4):
         at = pl.ds(offset_of(code, 1, h), wide, stride=R2)
-        here0, here1 = a0[at, :], a1[at, :]
-        first = jnp.where(head_tile_all(h, 0), here0, first)
-        second = jnp.where(head_tile_all(h, 1), here1, second)
-        if h < 3:
-            a0[at, :] = jnp.where(head_tile_all(h, 0), 0.0, here0)
-        if h > 1:
-            a1[at, :] = jnp.where(head_tile_all(h, 1) & (lanes() < 64), 0.0, here1)
+        first = jnp.where(head_tile_all(h, 0), a0[at, :], first)
+        second = jnp.where(head_tile_all(h, 1), a1[at, :], second)
     accw_ref[0] = first
     accw_ref[1] = second
-    one, two = normalised(a0[...], a1[...])
-    head, tail = packed(one, two)
+    one, two = normalised(both0, both1)
+    line = R1 * lax.broadcasted_iota(jnp.int32, (count, 1), 0)
+    mid0, mid1 = head_vectors([offset_of(code, 0, h) for h in range(4)])
+    far0, far1 = head_vectors([offset_of(code, 1, h) for h in range(4)])
+    gone0 = ((line + mid0) & (R2 - 1)) == far0
+    gone1 = ((line + mid1) & (R2 - 1)) == far1
+    head, tail = packed(jnp.where(gone0, 0.0, one), jnp.where(gone1, 0.0, two))
     out_ref[: head.shape[0]] = head
     out_ref[head.shape[0] :] = tail
 
@@ -264,15 +293,10 @@
     return [lax.rem(sub + step + subs, subs) for step in X_FROM]
 
 
-def final_kernel(offs_hbm, valid, w_ref, a0_ref, a1_ref, a2_ref, a3_ref, b0_ref, b1_ref, b2_ref, b3_ref,
-                 out_ref, f0, f1, wp, offsets, sem):
-    cols, rows = out_ref.shape
-    fetch = pltpu.make_async_copy(offs_hbm, offsets, sem)
-    fetch.start()
-    half, count, chunk = rows // 2, rows // R2, 256
-    sources = x_sources()
+def weights_kernel(w_ref, wp):
+    cols = w_ref.shape[1]
     wp[...] = jnp.zeros(wp.shape, BF16)
-    for i, source in enumerate(sources):
+    for i, source in enumerate(x_sources()):
         at = pl.ds(pl.multiple_of(source * cols, cols), cols)
         for part in (0, 1):
             for low, high in ((0, 128), (128, cols)):
@@ -280,6 +304,32 @@
                 wp[part, i * 256 : i * 256 + 128, low:high] = piece[:128]
                 tail = i * 256 + 128 + part * 64
                 wp[part, tail : tail + 64, low:high] = piece[128:]
+
+
+def add_rows(refs, wp, offsets, row, stride, f0, f1):
+    count = f0.shape[0] // stride
+    sources = x_sources()
+    for i, ref in enumerate(refs):
+        tail = ref[count:].astype(F32)
+        second = jnp.concatenate([tail, pltpu.roll(tail, 64, 1)], axis=0)
+        both = jnp.concatenate([ref[:count].astype(F32), second], axis=1)
+        stacked = jnp.concatenate(
+            [jnp.where(head_lanes(h) & (lanes(256) < 4 * HS), both, 0.0) for h in range(4)], axis=0
+        )
+        part = jnp.dot(stacked.astype(BF16), wp[0, i * 256 : (i + 1) * 256], preferred_element_type=F32)
+        for h in range(4):
+            at = pl.ds(offsets[row, sources[i] * 4 + h], count, stride=stride)
+            rows_h = slice(h * count, (h + 1) * count)
+            f0[at, :] = f0[at, :] + part[rows_h, :128]
+            f1[at, :] = f1[at, :] + part[rows_h, 128:]
+
+
+def base_kernel(offs_hbm, wp, a0_ref, a1_ref, a2_ref, a3_ref, m0_ref, m1_ref, m2_ref, m3_ref,
+                out_ref, f0, f1, offsets, sem):
+    fetch = pltpu.make_async_copy(offs_hbm, offsets, sem)
+    fetch.start()
+    rows = f0.shape[0]
+    half, chunk = rows // 2, 256
     for part in (0, 1):
         for start in range(0, half, chunk):
             at = slice(part * half + start, part * half + start + chunk)
@@ -291,19 +341,19 @@
             f0[at, :] = total[:, :128]
             f1[at, :] = total[:, 128:]
     fetch.wait()
-    for i, ref in enumerate((b0_ref, b1_ref, b2_ref, b3_ref)):
-        tail = ref[count:].astype(F32)
-        second = jnp.concatenate([tail, pltpu.roll(tail, 64, 1)], axis=0)
-        both = jnp.concatenate([ref[:count].astype(F32), second], axis=1)
-        stacked = jnp.concatenate(
-            [jnp.where(head_lanes(h) & (lanes(256) < 4 * HS), both, 0.0) for h in range(4)], axis=0
-        )
-        part = jnp.dot(stacked.astype(BF16), wp[0, i * 256 : (i + 1) * 256], preferred_element_type=F32)
-        for h in range(4):
-            at = pl.ds(offsets[1, sources[i] * 4 + h], count, stride=R2)
-            rows_h = slice(h * count, (h + 1) * count)
-            f0[at, :] = f0[at, :] + part[rows_h, :128]
-            f1[at, :] = f1[at, :] + part[rows_h, 128:]
+    add_rows((m0_ref, m1_ref, m2_ref, m3_ref), wp, offsets, 0, R1, f0, f1)
+    out_ref[0] = f0[...]
+    out_ref[1] = f1[...]
+
+
+def final_kernel(offs_hbm, valid, wp, base_ref, b0_ref, b1_ref, b2_ref, b3_ref, out_ref, f0, f1, offsets, sem):
+    cols, rows = out_ref.shape
+    fetch = pltpu.make_async_copy(offs_hbm, offsets, sem)
+    fetch.start()
+    f0[...] = base_ref[0]
+    f1[...] = base_ref[1]
+    fetch.wait()
+    add_rows((b0_ref, b1_ref, b2_ref, b3_ref), wp, offsets, 1, R2, f0, f1)
     position = lax.axis_index("seq") * rows + lax.broadcasted_iota(jnp.int32, (1, rows), 1)
     keep = position < valid[0]
     out_ref[:128, :] = jnp.where(keep, f0[...].T, 0.0).astype(BF16)
@@ -318,7 +368,7 @@
         body,
         out_shape=[jax.ShapeDtypeStruct(s, d) for s, d in outs],
         in_specs=[{"s": SMEM, "v": VMEM, "a": HBM}[kind] for kind in ins],
-        out_specs=[VMEM] * len(outs),
+        out_specs=[SMEM if d == jnp.int32 else VMEM for _, d in outs],
         scratch_shapes=[s if not isinstance(s, tuple) else pltpu.VMEM(*s) for s in scratch],
         cost_estimate=pl.CostEstimate(flops=int(flops), bytes_accessed=2 << 20, transcendentals=0),
         compiler_params=pltpu.CompilerParams(vmem_limit_bytes=limit << 20),
@@ -332,9 +382,6 @@
     n_sub = lax.axis_size("sub")
     n_chips = n_seq // 2
     mid, wide = rows // R1, rows // R2
-    shifts = 6 * lax.broadcasted_iota(jnp.int32, (2, 4), 1) + 2 * lax.broadcasted_iota(jnp.int32, (2, 4), 0)
-    mine = lax.dynamic_slice_in_dim(offsets, sub * 4, 4, 1)
-    code = (jnp.sum(jnp.left_shift(mine, shifts)) | (sub << 24)).reshape(1)
     w_cols = lax.dynamic_slice_in_dim(w_out, sub * cols, cols, 1)
 
     def along_z(value, up, down):
@@ -349,26 +396,30 @@
 
     smem_offsets = pltpu.SMEM(offsets.shape, jnp.int32)
     q_t, k_t, v_t = q_heads.T, k_heads.T, v_heads.T
-    near_q, w_cols = lax.optimization_barrier((q_t, w_cols))
-    kv_mid, kv_wide = call(
+    kv_mid, kv_wide, own_code = call(
         prep_kernel, "aaa",
-        [((mid, 384), BF16), ((wide, 384), BF16)],
+        [((mid, 384), BF16), ((wide, 384), BF16), ((1,), jnp.int32)],
         [((cols, rows), BF16)] * 2 + [smem_offsets] + [((rows, 128), F32)] * 3 + [pltpu.SemaphoreType.DMA((3,))],
         2e8, 60,
     )(offsets, k_t, v_t)
 
+    code = own_code | (sub << 24)
+    near_q, w_cols, code = lax.optimization_barrier((q_t, w_cols, code))
     four = n_chips // 4
     kv_both = flipped(kv_wide, 1)
     far_mid = flipped(kv_mid, 2)
     own_pair = jnp.concatenate([kv_wide, kv_both], axis=0)
     far4 = along_z(own_pair, four, -four)
-    acc, q_mid, q_wide = call(
-        near_kernel, "ssvvv",
-        [((2, rows, 128), F32), ((4 * mid, 256), BF16), ((4 * wide, 256), BF16)],
-        [((rows, 256), BF16), ((256, rows), BF16), ((256, rows), BF16)] + [((rows, 128), F32)] * 2,
+    packed_rows = rows + rows // 2
+    acc, q_mid, q_wide, attn = call(
+        near_kernel, "asvvv",
+        [((2, rows, 128), F32), ((4 * mid, 256), BF16), ((4 * wide, 256), BF16), ((packed_rows, 128), BF16)],
+        [((rows, 256), BF16), ((256, rows), BF16), ((256, rows), BF16)] + [((rows, 128), F32)] * 2
+        + [smem_offsets, pltpu.SemaphoreType.DMA],
         4e9, 28,
-    )(code, valid, near_q, k_t, v_t)
+    )(offsets, valid, near_q, k_t, v_t)
     far_mid, acc = lax.optimization_barrier((far_mid, acc))
+    attns = [along_x(attn, s) for s in (1, n_sub - 1, 2)]
 
     swap_mid = flipped(jnp.concatenate([kv_mid, far_mid], axis=0), 1)
     far8 = along_z(far4[:wide], four, -four)
@@ -376,13 +427,13 @@
     around2 = along_z(jnp.concatenate([own_pair, far4], axis=0), 2, -2)
     around_up = along_z(mine, 1, 1)
     around_down = along_z(mine, -1, -1)
-    attn, acc_wide = call(
+    attn_mid, acc_wide = call(
         functools.partial(middle_kernel, rows), "ssvvvvv",
-        [((rows + rows // 2, 128), BF16), ((2, wide, 128), F32)],
+        [((mid + mid // 2, 128), BF16), ((2, wide, 128), F32)],
         [((4 * mid, 256), BF16)] * 2 + [((rows, 128), F32)] * 2,
         1e9,
     )(code, valid, acc, q_mid, kv_mid, far_mid, swap_mid)
-    attns = [along_x(attn, s) for s in (1, n_sub - 1, 2)]
+    mids = [along_x(attn_mid, s) for s in (1, n_sub - 1, 2)]
 
     def wide_part(plan, acc_now, keys, last=False):
         n_keys = sum(k.shape[0] for k in keys)
@@ -400,12 +451,15 @@
     acc_wide = wide_part(((0, False), (0, True)), acc_wide, (early, early_other))
     acc_wide = wide_part(((1, False),), acc_wide, (late,))
     attn_wide = wide_part(((1, True),), acc_wide, (late_other,), last=True)
+    (w_blocks,) = call(weights_kernel, "v", [((2, 4 * 256, 256), BF16)], [], 1e7)(w_cols)
     wides = [along_x(attn_wide, s) for s in (1, n_sub - 1, 2)]
+    pair_of_tiles = [((rows, 128), F32)] * 2 + [smem_offsets, pltpu.SemaphoreType.DMA]
+    (base,) = call(
+        base_kernel, "av" + "v" * 8, [((2, rows, 128), F32)], pair_of_tiles, 1e9,
+    )(offsets, w_blocks, attn, *attns, attn_mid, *mids)
     (out,) = call(
-        final_kernel, "asv" + "v" * 8, [((cols, rows), BF16)],
-        [((rows, 128), F32)] * 2
-        + [((2, 4 * 256, 256), BF16), smem_offsets, pltpu.SemaphoreType.DMA], 1e9,
-    )(offsets, valid, w_cols, attn, *attns, attn_wide, *wides)
+        final_kernel, "asv" + "v" * 5, [((cols, rows), BF16)], pair_of_tiles, 5e8,
+    )(offsets, valid, w_blocks, base, attn_wide, *wides)
     return out.T
 
 

time: 91.3 us -> 90.8 us (level)
  waiting for transfers between devices: 17.7 us -> 4.54 us
  starting transfers between devices: 51.9 us -> 63.2 us
  Pallas kernels: 17.7 us -> 19.5 us
    ppermute x6 -> x9, waiting for transfers between devices: 9.6 us -> 1.49 us  [along_x(): lax.ppermute(value, 'sub', [(i, (i + step) % n_sub) for i in range(n_sub)])]
    ppermute x6 -> x9, starting transfers between devices: 11 us -> 17.4 us  [along_x(): lax.ppermute(value, 'sub', [(i, (i + step) % n_sub) for i in range(n_sub)])]
    ppermute x5, waiting for transfers between devices: 8.06 us -> 3.03 us  [along_z(): return lax.ppermute(value, 'seq', pairs)]
    ppermute x5, starting transfers between devices: 14.4 us -> 17.1 us  [along_z(): return lax.ppermute(value, 'seq', pairs)]
    ppermute x5, starting transfers between devices: 26.6 us -> 28.8 us  [flipped(): return lax.ppermute(value, 'seq', [(i, i ^ mask) for i in range(n_seq)])]
    pallas_call x4 -> x6, Pallas kernels: 14.6 us -> 16.3 us  [the longest x1 6.88 us: local(): call(near_kernel, 'asvvv', [((2, rows, 128), F32), ((4 * mid, 256), BF16)...]
  transfers between devices with their start and end apart: 16 -> 19, of which waited for: 5 -> 5; matrix products, arithmetic and copies ran while one was open for 1% -> 0% of each run, Pallas kernels for 14% -> 16%
where the time goes in v2:
time: 90.8 us; the launch traced here: 89.3 us
  starting transfers between devices  63.2 us (70%)
  Pallas kernels  19.5 us (21%)
  waiting for transfers between devices  4.54 us (5%)
  between operations  1.65 us (2%)
    ppermute x5, starting transfers between devices, flipped(): return lax.ppermute(value, 'seq', [(i, i ^ mask) for i in range(n_seq)])  28.8 us
    ppermute x9, starting transfers between devices, along_x(): lax.ppermute(value, 'sub', [(i, (i + step) % n_sub) for i in range(n_sub)])  17.4 us
    ppermute x5, starting transfers between devices, along_z(): return lax.ppermute(value, 'seq', pairs)  17.1 us
    pallas_call x1, Pallas kernels, local(): call(near_kernel, 'asvvv', [((2, rows, 128), F32), ((4 * mid, 256), BF16)...  6.88 us
    pallas_call x3, Pallas kernels, wide_part(): call(functools.partial(wide_kernel, rows, n_chips, plan, last), 'ssvv' +...  3.15 us
    ppermute x5, waiting for transfers between devices, along_z(): return lax.ppermute(value, 'seq', pairs)  3.03 us
    pallas_call x1, Pallas kernels, local(): call(prep_kernel, 'aaa', [((mid, 384), BF16), ((wide, 384), BF16), ((1,),...  2.49 us
    pallas_call x1, Pallas kernels, local(): call(functools.partial(middle_kernel, rows), 'ssvvvvv', [((mid + mid // 2...  2.47 us
  transfers between devices with their start and end apart: 19, of which 5 were waited for; matrix products, arithmetic and copies ran while one was open for 0% of the time, Pallas kernels for 16%

profile of v2, /device:TPU:33, one launch (start us, length us, event | category | flops | bytes accessed | tf_op | source)
XLA Modules:
  0.0 89.3 jit_solution(9874018654566940210)
XLA Ops:
  0.0 0.0 copy-start
  0.0 0.0 copy-start.1
  0.0 0.0 copy-start.2
  0.0 0.0 copy-start.4
  0.0 0.0 copy-start.5
  0.0 2.5 %shard_map.64 = (bf16[256,384]{1,0:T(8,128)(2,1)}, bf16[64,384]{1,0:T(8,128)(2,1)}, s32[1]{0:T(128)}) custom-call(s32[2,16]{1,0:T(2,128)} %offs_hbm.7, bf16[192,1024]{1,0:T(8,128)(2,1)} %bitcast.5, bf16[192,1024]{1,0:T(8,128)(2,1)} %bitcast.7), custom_call_target="tpu_custom_call" | custom-call | flops 200000000 | bytes 2097152 | tf_op jit(solution)/shard_map/pallas_call | solution.py:399
  2.5 20.5 %collective-permute-start.8 = (bf16[64,384]{1,0:T(8,128)(2,1)}, bf16[64,384]{1,0:T(8,128)(2,1)S(1)}, u32[]{:S(2)}, u32[]{:S(2)}) collective-permute-start(bf16[64,384]{1,0:T(8,128)(2,1)} %get-tuple-element.32), channel_id=1, source_target_pairs={{0,4},{4,0},{8,12},{12,8},{16,20},{20,16},{24,28},{28,24},{32,36},... | collective-permute-start | bytes 147464 | tf_op jit(solution)/shard_map/ppermute | solution.py:392
  23.1 0.0 collective-permute-start.3
  23.1 0.0 copy-done
  23.1 0.2 constant_dynamic-slice_fusion.w_ref
  24.5 0.0 copy-done.1
  24.5 0.0 copy-done.2
  24.5 0.0 copy-done.4
  24.5 0.0 copy-done.5
  24.5 0.0 copy-start.6
  24.6 6.9 %shard_map.66 = (f32[2,1024,128]{2,1,0:T(8,128)S(1)}, bf16[1024,256]{1,0:T(8,128)(2,1)S(1)}, bf16[256,256]{1,0:T(8,128)(2,1)S(1)}, bf16[1536,128]{1,0:T(8,128)(2,1)S(1)}) custom-call(s32[2,16]{1,0:T(2,128)S(1)} %copy-done.4, s32[1]{0:T(128)S(6)} %copy.13.valid, bf16[192,1024]{1,0:T(8,128)(2,1)S(1)} %bitcast.9, bf16[192,1024]{1,0:T(8,128)(2,1)S(1)} %bitcast.6, ...), custom_call_target="tpu_custom_call" | custom-call | flops 4000000000 | bytes 2097152 | tf_op jit(solution)/shard_map/pallas_call | solution.py:414
  31.4 0.0 copy-start.3
  31.4 0.1 collective-permute-start
  31.6 0.0 collective-permute-done.8
  31.6 0.0 copy-done.6
  31.6 4.9 %collective-permute-start.9 = (bf16[128,384]{1,0:T(8,128)(2,1)S(1)}, bf16[128,384]{1,0:T(8,128)(2,1)S(1)}, u32[]{:S(2)}, u32[]{:S(2)}) collective-permute-start(bf16[128,384]{1,0:T(8,128)(2,1)S(1)} %pad_maximum_fusion.2), channel_id=1, source_target_pairs={{0,32},{4,100},{8,40},{12,108},{16,48},{20,116},{24,56},{28,124},{... | collective-permute-start | bytes 294920 | tf_op jit(solution)/shard_map/ppermute | solution.py:389
  36.5 2.9 %collective-permute-done.9 = bf16[128,384]{1,0:T(8,128)(2,1)S(1)} collective-permute-done((bf16[128,384]{1,0:T(8,128)(2,1)S(1)}, bf16[128,384]{1,0:T(8,128)(2,1)S(1)}, u32[]{:S(2)}, u32[]{:S(2)}) %collective-permute-start.9) | collective-permute-done | bytes 98336 | tf_op jit(solution)/shard_map/ppermute | solution.py:389
  39.4 5.2 %collective-permute-start.10 = (bf16[64,384]{1,0:T(8,128)(2,1)S(1)}, bf16[64,384]{1,0:T(8,128)(2,1)S(1)}, u32[]{:S(2)}, u32[]{:S(2)}) collective-permute-start(bf16[64,384]{1,0:T(8,128)(2,1)S(1)} %slice.4), channel_id=1, source_target_pairs={{0,32},{4,100},{8,40},{12,108},{16,48},{20,116},{24,56},{28,124},{... | collective-permute-start | bytes 147464 | tf_op jit(solution)/shard_map/ppermute | solution.py:389
  44.6 1.5 %collective-permute-start.11 = (bf16[256,384]{1,0:T(8,128)(2,1)S(1)}, bf16[256,384]{1,0:T(8,128)(2,1)S(1)}, u32[]{:S(2)}, u32[]{:S(2)}) collective-permute-start(bf16[256,384]{1,0:T(8,128)(2,1)S(1)} %pad_maximum_fusion.1), channel_id=1, source_target_pairs={{0,16},{4,116},{8,24},{12,124},{16,32},{20,4},{24,40},{28,12},{32,... | collective-permute-start | bytes 589832 | tf_op jit(solution)/shard_map/ppermute | solution.py:389
  46.2 0.1 collective-permute-done.10
  46.3 2.1 %collective-permute-start.13 = (bf16[256,384]{1,0:T(8,128)(2,1)S(1)}, bf16[256,384]{1,0:T(8,128)(2,1)S(1)}, u32[]{:S(2)}, u32[]{:S(2)}) collective-permute-start(bf16[256,384]{1,0:T(8,128)(2,1)S(1)} %get-tuple-element.35), channel_id=1, source_target_pairs={{0,8},{4,12},{8,16},{12,20},{16,24},{20,28},{24,32},{28,36},{32,40... | collective-permute-start | bytes 589832 | tf_op jit(solution)/shard_map/ppermute | solution.py:389
  48.4 3.4 %collective-permute-start.14 = (bf16[256,384]{1,0:T(8,128)(2,1)S(1)}, bf16[256,384]{1,0:T(8,128)(2,1)S(1)}, u32[]{:S(2)}, u32[]{:S(2)}) collective-permute-start(bf16[256,384]{1,0:T(8,128)(2,1)S(1)} %get-tuple-element.35), channel_id=1, source_target_pairs={{0,120},{4,124},{8,0},{12,4},{16,8},{20,12},{24,16},{28,20},{32,24... | collective-permute-start | bytes 589832 | tf_op jit(solution)/shard_map/ppermute | solution.py:389
  51.8 0.0 collective-permute-done.3.far_ref
  51.8 0.0 copy-done.3
  51.8 4.8 %collective-permute-start.4 = (bf16[512,384]{1,0:T(8,128)(2,1)S(1)}, bf16[512,384]{1,0:T(8,128)(2,1)S(1)}, u32[]{:S(2)}, u32[]{:S(2)}) collective-permute-start(bf16[512,384]{1,0:T(8,128)(2,1)S(1)} %pad_maximum_fusion), channel_id=1, source_target_pairs={{0,4},{4,0},{8,12},{12,8},{16,20},{20,16},{24,28},{28,24},{32,36},... | collective-permute-start | bytes 1179656 | tf_op jit(solution)/shard_map/ppermute | solution.py:392
  56.6 0.0 collective-permute-done.11
  56.7 0.3 collective-permute-start.12
  57.0 0.0 collective-permute-done.13
  57.1 0.1 collective-permute-done.14
  57.2 3.0 %collective-permute-start.15 = (bf16[512,384]{1,0:T(8,128)(2,1)S(1)}, bf16[512,384]{1,0:T(8,128)(2,1)S(1)}, u32[]{:S(2)}, u32[]{:S(2)}) collective-permute-start(bf16[512,384]{1,0:T(8,128)(2,1)S(1)} %constant_dynamic-update-slice_fusion.7.refs_0_), channel_id=1, source_target_pairs={{0,4},{4,0},{8,12},{12,8},{16,20},{20,16},{24,28},{28,24},{32,36},... | collective-permute-start | bytes 1179656 | tf_op jit(solution)/shard_map/ppermute | solution.py:392
  60.2 1.7 %collective-permute-start.1 = (bf16[1536,128]{1,0:T(8,128)(2,1)S(1)}, bf16[1536,128]{1,0:T(8,128)(2,1)S(1)}, u32[]{:S(2)}, u32[]{:S(2)}) collective-permute-start(bf16[1536,128]{1,0:T(8,128)(2,1)S(1)} %get-tuple-element.22.a0_ref), channel_id=1, source_target_pairs={{0,3},{1,0},{2,1},{3,2},{4,7},{5,4},{6,5},{7,6},{8,11},{9,8},{10,9... | collective-permute-start | bytes 1179656 | tf_op jit(solution)/shard_map/ppermute | solution.py:395
  61.9 0.0 collective-permute-done.4.swap_ref
  61.9 2.0 %collective-permute-start.2 = (bf16[1536,128]{1,0:T(8,128)(2,1)S(1)}, bf16[1536,128]{1,0:T(8,128)(2,1)S(1)}, u32[]{:S(2)}, u32[]{:S(2)}) collective-permute-start(bf16[1536,128]{1,0:T(8,128)(2,1)S(1)} %get-tuple-element.22.a0_ref), channel_id=1, source_target_pairs={{0,2},{1,3},{2,0},{3,1},{4,6},{5,7},{6,4},{7,5},{8,10},{9,11},{10,... | collective-permute-start | bytes 1179656 | tf_op jit(solution)/shard_map/ppermute | solution.py:395
  63.9 0.2 shard_map.65.wp
  64.1 2.5 %shard_map.67 = (bf16[384,128]{1,0:T(8,128)(2,1)S(1)}, f32[2,64,128]{2,1,0:T(8,128)S(1)}) custom-call(s32[1]{0:T(128)S(6)} %or.7.code, s32[1]{0:T(128)S(6)} %copy.13.valid, f32[2,1024,128]{2,1,0:T(8,128)S(1)} %get-tuple-element.26.acc_ref, bf16[1024,256]{1,0:T(8,128)(2,1)S(1)} %get-tuple-element.27.qm_ref, bf16[256,384]{1,0:T(8,128)(2,1)S(1)} %copy-done.3, ...), custom_call_target="tpu_custom_call" | custom-call | flops 1000000000 | bytes 2097152 | tf_op jit(solution)/shard_map/pallas_call | solution.py:430
  66.5 0.0 collective-permute-done.a1_ref
  66.5 0.6 collective-permute-start.5
  67.1 0.0 collective-permute-done.12.refs_1_
  67.1 2.2 %collective-permute-start.6 = (bf16[384,128]{1,0:T(8,128)(2,1)S(1)}, bf16[384,128]{1,0:T(8,128)(2,1)S(1)}, u32[]{:S(2)}, u32[]{:S(2)}) collective-permute-start(bf16[384,128]{1,0:T(8,128)(2,1)S(1)} %get-tuple-element.29.m0_ref), channel_id=1, source_target_pairs={{0,3},{1,0},{2,1},{3,2},{4,7},{5,4},{6,5},{7,6},{8,11},{9,8},{10,9... | collective-permute-start | bytes 294920 | tf_op jit(solution)/shard_map/ppermute | solution.py:395
  69.3 0.0 collective-permute-done.15.refs_0_
  69.3 0.0 collective-permute-start.7
  69.3 1.2 %shard_map.69.accw_ref = f32[2,64,128]{2,1,0:T(8,128)S(1)} custom-call(s32[1]{0:T(128)S(6)} %or.7.code, s32[1]{0:T(128)S(6)} %copy.13.valid, bf16[256,256]{1,0:T(8,128)(2,1)S(1)} %get-tuple-element.30.qw_ref, f32[2,64,128]{2,1,0:T(8,128)S(1)} %get-tuple-element.31.accw_ref, bf16[512,384]{1,0:T(8,128)(2,1)S(1)} %constant_dynamic-update-slice_fusion.refs_0_, ...), custom_call_target="tpu_custom_call" | custom-call | flops 500000000 | bytes 2097152 | tf_op jit(solution)/shard_map/pallas_call | solution.py:440
  70.5 0.9 %shard_map.70.accw_ref = f32[2,64,128]{2,1,0:T(8,128)S(1)} custom-call(s32[1]{0:T(128)S(6)} %or.7.code, s32[1]{0:T(128)S(6)} %copy.13.valid, bf16[256,256]{1,0:T(8,128)(2,1)S(1)} %get-tuple-element.30.qw_ref, f32[2,64,128]{2,1,0:T(8,128)S(1)} %shard_map.69.accw_ref, bf16[512,384]{1,0:T(8,128)(2,1)S(1)} %constant_dynamic-update-slice_fusion.7.refs_0_), custom_call_target="tpu_custom_call" | custom-call | flops 500000000 | bytes 2097152 | tf_op jit(solution)/shard_map/pallas_call | solution.py:440
  71.4 1.1 %shard_map.71.b0_ref = bf16[96,128]{1,0:T(8,128)(2,1)S(1)} custom-call(s32[1]{0:T(128)S(6)} %or.7.code, s32[1]{0:T(128)S(6)} %copy.13.valid, bf16[256,256]{1,0:T(8,128)(2,1)S(1)} %get-tuple-element.30.qw_ref, f32[2,64,128]{2,1,0:T(8,128)S(1)} %shard_map.70.accw_ref, bf16[512,384]{1,0:T(8,128)(2,1)S(1)} %collective-permute-done.15.refs_0_), custom_call_target="tpu_custom_call" | custom-call | flops 500000000 | bytes 2097152 | tf_op jit(solution)/shard_map/pallas_call | solution.py:440
  72.5 0.0 collective-permute-done.1.a2_ref
  72.5 0.8 collective-permute-start.16
  73.3 0.4 collective-permute-done.2.a3_ref
  73.7 8.6 %collective-permute-start.17 = (bf16[96,128]{1,0:T(8,128)(2,1)S(1)}, bf16[96,128]{1,0:T(8,128)(2,1)S(1)}, u32[]{:S(2)}, u32[]{:S(2)}) collective-permute-start(bf16[96,128]{1,0:T(8,128)(2,1)S(1)} %shard_map.71.b0_ref), channel_id=1, source_target_pairs={{0,3},{1,0},{2,1},{3,2},{4,7},{5,4},{6,5},{7,6},{8,11},{9,8},{10,9... | collective-permute-start | bytes 73736 | tf_op jit(solution)/shard_map/ppermute | solution.py:395
  82.3 0.0 collective-permute-done.5.m1_ref
  82.3 1.4 %collective-permute-start.18 = (bf16[96,128]{1,0:T(8,128)(2,1)S(1)}, bf16[96,128]{1,0:T(8,128)(2,1)S(1)}, u32[]{:S(2)}, u32[]{:S(2)}) collective-permute-start(bf16[96,128]{1,0:T(8,128)(2,1)S(1)} %shard_map.71.b0_ref), channel_id=1, source_target_pairs={{0,2},{1,3},{2,0},{3,1},{4,6},{5,7},{6,4},{7,5},{8,10},{9,11},{10,... | collective-permute-start | bytes 73736 | tf_op jit(solution)/shard_map/ppermute | solution.py:395
  83.7 0.0 collective-permute-done.6.m2_ref
  83.7 0.0 collective-permute-done.7.m3_ref
  83.7 1.9 %shard_map.68.base_ref = f32[2,1024,128]{2,1,0:T(8,128)S(1)} custom-call(s32[2,16]{1,0:T(2,128)S(1)} %copy-done.4, bf16[2,1024,256]{2,1,0:T(8,128)(2,1)S(1)} %shard_map.65.wp, bf16[1536,128]{1,0:T(8,128)(2,1)S(1)} %get-tuple-element.22.a0_ref, bf16[1536,128]{1,0:T(8,128)(2,1)S(1)} %collective-permute-done.a1_ref, ...), custom_call_target="tpu_custom_call" | custom-call | flops 1000000000 | bytes 2097152 | tf_op jit(solution)/shard_map/pallas_call | solution.py:457
  85.6 0.0 collective-permute-done.16.b1_ref
  85.6 0.0 collective-permute-done.17.b2_ref
  85.6 1.1 %collective-permute-done.18.b3_ref = bf16[96,128]{1,0:T(8,128)(2,1)S(1)} collective-permute-done((bf16[96,128]{1,0:T(8,128)(2,1)S(1)}, bf16[96,128]{1,0:T(8,128)(2,1)S(1)}, u32[]{:S(2)}, u32[]{:S(2)}) %collective-permute-start.18) | collective-permute-done | bytes 24608 | tf_op jit(solution)/shard_map/ppermute | solution.py:395
  86.7 2.4 %shard_map.72 = bf16[192,1024]{1,0:T(8,128)(2,1)} custom-call(s32[2,16]{1,0:T(2,128)S(1)} %copy-done.4, s32[1]{0:T(128)S(6)} %copy.13.valid, bf16[2,1024,256]{2,1,0:T(8,128)(2,1)S(1)} %shard_map.65.wp, f32[2,1024,128]{2,1,0:T(8,128)S(1)} %shard_map.68.base_ref, bf16[96,128]{1,0:T(8,128)(2,1)S(1)} %shard_map.71.b0_ref, ...), custom_call_target="tpu_custom_call" | custom-call | flops 500000000 | bytes 2097152 | tf_op jit(solution)/shard_map/pallas_call | solution.py:460
  (10 shorter events, 0.2 us)
Async XLA Ops:
  0.0 23.1 %copy-start = (bf16[768,768]{1,0:T(8,128)(2,1)S(1)}, bf16[768,768]{1,0:T(8,128)(2,1)}, u32[]{:S(2)}) copy-start(bf16[768,768]{1,0:T(8,128)(2,1)} %param.9) | copy-start | bytes 3538948
  0.0 24.5 %copy-start.1 = (bf16[1024,192]{0,1:T(8,128)(2,1)S(1)}, bf16[1024,192]{0,1:T(8,128)(2,1)}, u32[]{:S(2)}) copy-start(bf16[1024,192]{0,1:T(8,128)(2,1)} %param.7) | copy-start | bytes 1179652
  0.0 24.5 %copy-start.2 = (bf16[1024,192]{0,1:T(8,128)(2,1)S(1)}, bf16[1024,192]{0,1:T(8,128)(2,1)}, u32[]{:S(2)}) copy-start(bf16[1024,192]{0,1:T(8,128)(2,1)} %param.8) | copy-start | bytes 1179652
  0.0 24.5 %copy-start.4 = (s32[2,16]{1,0:T(2,128)S(1)}, s32[2,16]{1,0:T(2,128)}, u32[]{:S(2)}) copy-start(s32[2,16]{1,0:T(2,128)} %offs_hbm.7) | copy-start | bytes 388
  0.0 24.5 %copy-start.5 = (bf16[1024,192]{0,1:T(8,128)(2,1)S(1)}, bf16[1024,192]{0,1:T(8,128)(2,1)}, u32[]{:S(2)}) copy-start(bf16[1024,192]{0,1:T(8,128)(2,1)} %param.6) | copy-start | bytes 1179652
  2.5 29.1 %collective-permute-start.8 = (bf16[64,384]{1,0:T(8,128)(2,1)}, bf16[64,384]{1,0:T(8,128)(2,1)S(1)}, u32[]{:S(2)}, u32[]{:S(2)}) collective-permute-start(bf16[64,384]{1,0:T(8,128)(2,1)} %get-tuple-element.32), channel_id=1, source_target_pairs={{0,4},{4,0},{8,12},{12,8},{16,20},{20,16},{24,28},{28,24},{32,36},... | collective-permute-start | bytes 147464 | tf_op jit(solution)/shard_map/ppermute | solution.py:392
  23.1 28.7 %collective-permute-start.3 = (bf16[256,384]{1,0:T(8,128)(2,1)}, bf16[256,384]{1,0:T(8,128)(2,1)S(1)}, u32[]{:S(2)}, u32[]{:S(2)}) collective-permute-start(bf16[256,384]{1,0:T(8,128)(2,1)} %get-tuple-element.24.own_ref), channel_id=1, source_target_pairs={{0,8},{4,12},{8,0},{12,4},{16,24},{20,28},{24,16},{28,20},{32,40},... | collective-permute-start | bytes 589832 | tf_op jit(solution)/shard_map/ppermute | solution.py:392
  24.5 7.1 %copy-start.6 = (bf16[64,384]{1,0:T(8,128)(2,1)S(1)}, bf16[64,384]{1,0:T(8,128)(2,1)}, u32[]{:S(2)}) copy-start(bf16[64,384]{1,0:T(8,128)(2,1)} %get-tuple-element.32) | copy-start | bytes 147460
  31.4 20.3 %copy-start.3 = (bf16[256,384]{1,0:T(8,128)(2,1)S(1)}, bf16[256,384]{1,0:T(8,128)(2,1)}, u32[]{:S(2)}) copy-start(bf16[256,384]{1,0:T(8,128)(2,1)} %get-tuple-element.24.own_ref) | copy-start | bytes 589828
  31.4 35.1 %collective-permute-start = (bf16[1536,128]{1,0:T(8,128)(2,1)S(1)}, bf16[1536,128]{1,0:T(8,128)(2,1)S(1)}, u32[]{:S(2)}, u32[]{:S(2)}) collective-permute-start(bf16[1536,128]{1,0:T(8,128)(2,1)S(1)} %get-tuple-element.22.a0_ref), channel_id=1, source_target_pairs={{0,1},{1,2},{2,3},{3,0},{4,5},{5,6},{6,7},{7,4},{8,9},{9,10},{10,1... | collective-permute-start | bytes 1179656 | tf_op jit(solution)/shard_map/ppermute | solution.py:395
  31.6 7.8 %collective-permute-start.9 = (bf16[128,384]{1,0:T(8,128)(2,1)S(1)}, bf16[128,384]{1,0:T(8,128)(2,1)S(1)}, u32[]{:S(2)}, u32[]{:S(2)}) collective-permute-start(bf16[128,384]{1,0:T(8,128)(2,1)S(1)} %pad_maximum_fusion.2), channel_id=1, source_target_pairs={{0,32},{4,100},{8,40},{12,108},{16,48},{20,116},{24,56},{28,124},{... | collective-permute-start | bytes 294920 | tf_op jit(solution)/shard_map/ppermute | solution.py:389
  39.4 6.9 %collective-permute-start.10 = (bf16[64,384]{1,0:T(8,128)(2,1)S(1)}, bf16[64,384]{1,0:T(8,128)(2,1)S(1)}, u32[]{:S(2)}, u32[]{:S(2)}) collective-permute-start(bf16[64,384]{1,0:T(8,128)(2,1)S(1)} %slice.4), channel_id=1, source_target_pairs={{0,32},{4,100},{8,40},{12,108},{16,48},{20,116},{24,56},{28,124},{... | collective-permute-start | bytes 147464 | tf_op jit(solution)/shard_map/ppermute | solution.py:389
  44.6 12.0 %collective-permute-start.11 = (bf16[256,384]{1,0:T(8,128)(2,1)S(1)}, bf16[256,384]{1,0:T(8,128)(2,1)S(1)}, u32[]{:S(2)}, u32[]{:S(2)}) collective-permute-start(bf16[256,384]{1,0:T(8,128)(2,1)S(1)} %pad_maximum_fusion.1), channel_id=1, source_target_pairs={{0,16},{4,116},{8,24},{12,124},{16,32},{20,4},{24,40},{28,12},{32,... | collective-permute-start | bytes 589832 | tf_op jit(solution)/shard_map/ppermute | solution.py:389
  46.3 10.7 %collective-permute-start.13 = (bf16[256,384]{1,0:T(8,128)(2,1)S(1)}, bf16[256,384]{1,0:T(8,128)(2,1)S(1)}, u32[]{:S(2)}, u32[]{:S(2)}) collective-permute-start(bf16[256,384]{1,0:T(8,128)(2,1)S(1)} %get-tuple-element.35), channel_id=1, source_target_pairs={{0,8},{4,12},{8,16},{12,20},{16,24},{20,28},{24,32},{28,36},{32,40... | collective-permute-start | bytes 589832 | tf_op jit(solution)/shard_map/ppermute | solution.py:389
  48.4 8.7 %collective-permute-start.14 = (bf16[256,384]{1,0:T(8,128)(2,1)S(1)}, bf16[256,384]{1,0:T(8,128)(2,1)S(1)}, u32[]{:S(2)}, u32[]{:S(2)}) collective-permute-start(bf16[256,384]{1,0:T(8,128)(2,1)S(1)} %get-tuple-element.35), channel_id=1, source_target_pairs={{0,120},{4,124},{8,0},{12,4},{16,8},{20,12},{24,16},{28,20},{32,24... | collective-permute-start | bytes 589832 | tf_op jit(solution)/shard_map/ppermute | solution.py:389
  51.8 10.1 %collective-permute-start.4 = (bf16[512,384]{1,0:T(8,128)(2,1)S(1)}, bf16[512,384]{1,0:T(8,128)(2,1)S(1)}, u32[]{:S(2)}, u32[]{:S(2)}) collective-permute-start(bf16[512,384]{1,0:T(8,128)(2,1)S(1)} %pad_maximum_fusion), channel_id=1, source_target_pairs={{0,4},{4,0},{8,12},{12,8},{16,20},{20,16},{24,28},{28,24},{32,36},... | collective-permute-start | bytes 1179656 | tf_op jit(solution)/shard_map/ppermute | solution.py:392
  56.7 10.4 %collective-permute-start.12 = (bf16[512,384]{1,0:T(8,128)(2,1)S(1)}, bf16[512,384]{1,0:T(8,128)(2,1)S(1)}, u32[]{:S(2)}, u32[]{:S(2)}) collective-permute-start(bf16[512,384]{1,0:T(8,128)(2,1)S(1)} %constant_dynamic-update-slice_fusion.refs_0_), channel_id=1, source_target_pairs={{0,4},{4,0},{8,12},{12,8},{16,20},{20,16},{24,28},{28,24},{32,36},... | collective-permute-start | bytes 1179656 | tf_op jit(solution)/shard_map/ppermute | solution.py:392
  57.2 12.2 %collective-permute-start.15 = (bf16[512,384]{1,0:T(8,128)(2,1)S(1)}, bf16[512,384]{1,0:T(8,128)(2,1)S(1)}, u32[]{:S(2)}, u32[]{:S(2)}) collective-permute-start(bf16[512,384]{1,0:T(8,128)(2,1)S(1)} %constant_dynamic-update-slice_fusion.7.refs_0_), channel_id=1, source_target_pairs={{0,4},{4,0},{8,12},{12,8},{16,20},{20,16},{24,28},{28,24},{32,36},... | collective-permute-start | bytes 1179656 | tf_op jit(solution)/shard_map/ppermute | solution.py:392
  60.2 12.3 %collective-permute-start.1 = (bf16[1536,128]{1,0:T(8,128)(2,1)S(1)}, bf16[1536,128]{1,0:T(8,128)(2,1)S(1)}, u32[]{:S(2)}, u32[]{:S(2)}) collective-permute-start(bf16[1536,128]{1,0:T(8,128)(2,1)S(1)} %get-tuple-element.22.a0_ref), channel_id=1, source_target_pairs={{0,3},{1,0},{2,1},{3,2},{4,7},{5,4},{6,5},{7,6},{8,11},{9,8},{10,9... | collective-permute-start | bytes 1179656 | tf_op jit(solution)/shard_map/ppermute | solution.py:395
  61.9 11.8 %collective-permute-start.2 = (bf16[1536,128]{1,0:T(8,128)(2,1)S(1)}, bf16[1536,128]{1,0:T(8,128)(2,1)S(1)}, u32[]{:S(2)}, u32[]{:S(2)}) collective-permute-start(bf16[1536,128]{1,0:T(8,128)(2,1)S(1)} %get-tuple-element.22.a0_ref), channel_id=1, source_target_pairs={{0,2},{1,3},{2,0},{3,1},{4,6},{5,7},{6,4},{7,5},{8,10},{9,11},{10,... | collective-permute-start | bytes 1179656 | tf_op jit(solution)/shard_map/ppermute | solution.py:395
  66.5 15.8 %collective-permute-start.5 = (bf16[384,128]{1,0:T(8,128)(2,1)S(1)}, bf16[384,128]{1,0:T(8,128)(2,1)S(1)}, u32[]{:S(2)}, u32[]{:S(2)}) collective-permute-start(bf16[384,128]{1,0:T(8,128)(2,1)S(1)} %get-tuple-element.29.m0_ref), channel_id=1, source_target_pairs={{0,1},{1,2},{2,3},{3,0},{4,5},{5,6},{6,7},{7,4},{8,9},{9,10},{10,1... | collective-permute-start | bytes 294920 | tf_op jit(solution)/shard_map/ppermute | solution.py:395
  67.1 16.6 %collective-permute-start.6 = (bf16[384,128]{1,0:T(8,128)(2,1)S(1)}, bf16[384,128]{1,0:T(8,128)(2,1)S(1)}, u32[]{:S(2)}, u32[]{:S(2)}) collective-permute-start(bf16[384,128]{1,0:T(8,128)(2,1)S(1)} %get-tuple-element.29.m0_ref), channel_id=1, source_target_pairs={{0,3},{1,0},{2,1},{3,2},{4,7},{5,4},{6,5},{7,6},{8,11},{9,8},{10,9... | collective-permute-start | bytes 294920 | tf_op jit(solution)/shard_map/ppermute | solution.py:395
  69.3 14.3 %collective-permute-start.7 = (bf16[384,128]{1,0:T(8,128)(2,1)S(1)}, bf16[384,128]{1,0:T(8,128)(2,1)S(1)}, u32[]{:S(2)}, u32[]{:S(2)}) collective-permute-start(bf16[384,128]{1,0:T(8,128)(2,1)S(1)} %get-tuple-element.29.m0_ref), channel_id=1, source_target_pairs={{0,2},{1,3},{2,0},{3,1},{4,6},{5,7},{6,4},{7,5},{8,10},{9,11},{10,... | collective-permute-start | bytes 294920 | tf_op jit(solution)/shard_map/ppermute | solution.py:395
  72.5 13.1 %collective-permute-start.16 = (bf16[96,128]{1,0:T(8,128)(2,1)S(1)}, bf16[96,128]{1,0:T(8,128)(2,1)S(1)}, u32[]{:S(2)}, u32[]{:S(2)}) collective-permute-start(bf16[96,128]{1,0:T(8,128)(2,1)S(1)} %shard_map.71.b0_ref), channel_id=1, source_target_pairs={{0,1},{1,2},{2,3},{3,0},{4,5},{5,6},{6,7},{7,4},{8,9},{9,10},{10,1... | collective-permute-start | bytes 73736 | tf_op jit(solution)/shard_map/ppermute | solution.py:395
  73.7 11.9 %collective-permute-start.17 = (bf16[96,128]{1,0:T(8,128)(2,1)S(1)}, bf16[96,128]{1,0:T(8,128)(2,1)S(1)}, u32[]{:S(2)}, u32[]{:S(2)}) collective-permute-start(bf16[96,128]{1,0:T(8,128)(2,1)S(1)} %shard_map.71.b0_ref), channel_id=1, source_target_pairs={{0,3},{1,0},{2,1},{3,2},{4,7},{5,4},{6,5},{7,6},{8,11},{9,8},{10,9... | collective-permute-start | bytes 73736 | tf_op jit(solution)/shard_map/ppermute | solution.py:395
  82.3 4.4 %collective-permute-start.18 = (bf16[96,128]{1,0:T(8,128)(2,1)S(1)}, bf16[96,128]{1,0:T(8,128)(2,1)S(1)}, u32[]{:S(2)}, u32[]{:S(2)}) collective-permute-start(bf16[96,128]{1,0:T(8,128)(2,1)S(1)} %shard_map.71.b0_ref), channel_id=1, source_target_pairs={{0,2},{1,3},{2,0},{3,1},{4,6},{5,7},{6,4},{7,5},{8,10},{9,11},{10,... | collective-permute-start | bytes 73736 | tf_op jit(solution)/shard_map/ppermute | solution.py:395

commit v3 on v1

--- a/solution.py
+++ b/solution.py
@@ -56,7 +56,7 @@
     return peak * LOG2_SCALE, out
 
 
-def prep_kernel(offs_hbm, k_hbm, v_hbm, mid_ref, wide_ref, k_ref, v_ref, offsets, kf, vf, tf, sems):
+def prep_kernel(offs_hbm, k_hbm, v_hbm, mid_ref, wide_ref, code_ref, k_ref, v_ref, offsets, kf, vf, tf, sems):
     copies = [
         pltpu.make_async_copy(source, target, sems.at[i])
         for i, (source, target) in enumerate(
@@ -72,6 +72,9 @@
     vf[...] = v_ref[:128, :].astype(F32).T
     tf[...] = jnp.concatenate([k_ref[128:192, :], v_ref[128:192, :]], axis=0).astype(F32).T
     copies[0].wait()
+    code_ref[0] = sum(
+        offsets[row, first_head + h] << (6 * h + 2 * row) for row in range(2) for h in range(4)
+    )
     lane = lanes()
     for row, stride, out in ((0, R1, mid_ref), (1, R2, wide_ref)):
         count = out.shape[0]
@@ -86,8 +89,11 @@
         out[:, 256:384] = joined.astype(BF16)
 
 
-def near_kernel(code, valid, q_ref, k_ref, v_ref, acc_ref, qm_ref, qw_ref, qa, ka, va, q0, q1):
+def near_kernel(offs_hbm, valid, q_ref, k_ref, v_ref, acc_ref, qm_ref, qw_ref, qa, ka, va, q0, q1, offsets, sem):
     rows = q_ref.shape[1]
+    fetch = pltpu.make_async_copy(offs_hbm, offsets, sem)
+    fetch.start()
+    first_head = lax.axis_index("sub") * 4
     start = lax.axis_index("seq") * rows
     line = lax.broadcasted_iota(jnp.int32, (64, 1), 0)
     ones = jnp.broadcast_to(jnp.where(line < 4, 1.0, 0.0), (64, rows))
@@ -101,14 +107,6 @@
     ka[192:256, :] = jnp.where(line < 4, dead, 0.0).astype(BF16)
     va[:192, :] = v_ref[...]
     va[192:256, :] = ones.astype(BF16)
-
-    for row, stride, out in ((0, R1, qm_ref), (1, R2, qw_ref)):
-        count = rows // stride
-        for h in range(4):
-            for tile, ref in ((0, q0), (1, q1)):
-                picked = ref[pl.ds(offset_of(code, row, h), count, stride=stride), :]
-                picked = jnp.where(head_tile(h, tile), picked, 0.0)
-                out[h * count : (h + 1) * count, tile * 128 : (tile + 1) * 128] = picked.astype(BF16)
 
     chunk = 512
 
@@ -136,6 +134,15 @@
         return carry
 
     lax.fori_loop(0, rows // chunk, step, 0)
+
+    fetch.wait()
+    for row, stride, out in ((0, R1, qm_ref), (1, R2, qw_ref)):
+        count = rows // stride
+        for h in range(4):
+            for tile, ref in ((0, q0), (1, q1)):
+                picked = ref[pl.ds(offsets[row, first_head + h], count, stride=stride), :]
+                picked = jnp.where(head_tile(h, tile), picked, 0.0)
+                out[h * count : (h + 1) * count, tile * 128 : (tile + 1) * 128] = picked.astype(BF16)
 
 
 def open_piece(piece, first, stride, code, row, valid, ka, va, at):
@@ -264,15 +271,10 @@
     return [lax.rem(sub + step + subs, subs) for step in X_FROM]
 
 
-def final_kernel(offs_hbm, valid, w_ref, a0_ref, a1_ref, a2_ref, a3_ref, b0_ref, b1_ref, b2_ref, b3_ref,
-                 out_ref, f0, f1, wp, offsets, sem):
-    cols, rows = out_ref.shape
-    fetch = pltpu.make_async_copy(offs_hbm, offsets, sem)
-    fetch.start()
-    half, count, chunk = rows // 2, rows // R2, 256
-    sources = x_sources()
+def weights_kernel(w_ref, wp):
+    cols = w_ref.shape[1]
     wp[...] = jnp.zeros(wp.shape, BF16)
-    for i, source in enumerate(sources):
+    for i, source in enumerate(x_sources()):
         at = pl.ds(pl.multiple_of(source * cols, cols), cols)
         for part in (0, 1):
             for low, high in ((0, 128), (128, cols)):
@@ -280,6 +282,15 @@
                 wp[part, i * 256 : i * 256 + 128, low:high] = piece[:128]
                 tail = i * 256 + 128 + part * 64
                 wp[part, tail : tail + 64, low:high] = piece[128:]
+
+
+def final_kernel(offs_hbm, valid, wp, a0_ref, a1_ref, a2_ref, a3_ref, b0_ref, b1_ref, b2_ref, b3_ref,
+                 out_ref, f0, f1, offsets, sem):
+    cols, rows = out_ref.shape
+    fetch = pltpu.make_async_copy(offs_hbm, offsets, sem)
+    fetch.start()
+    half, count, chunk = rows // 2, rows // R2, 256
+    sources = x_sources()
     for part in (0, 1):
         for start in range(0, half, chunk):
             at = slice(part * half + start, part * half + start + chunk)
@@ -318,7 +329,7 @@
         body,
         out_shape=[jax.ShapeDtypeStruct(s, d) for s, d in outs],
         in_specs=[{"s": SMEM, "v": VMEM, "a": HBM}[kind] for kind in ins],
-        out_specs=[VMEM] * len(outs),
+        out_specs=[SMEM if d == jnp.int32 else VMEM for _, d in outs],
         scratch_shapes=[s if not isinstance(s, tuple) else pltpu.VMEM(*s) for s in scratch],
         cost_estimate=pl.CostEstimate(flops=int(flops), bytes_accessed=2 << 20, transcendentals=0),
         compiler_params=pltpu.CompilerParams(vmem_limit_bytes=limit << 20),
@@ -332,9 +343,6 @@
     n_sub = lax.axis_size("sub")
     n_chips = n_seq // 2
     mid, wide = rows // R1, rows // R2
-    shifts = 6 * lax.broadcasted_iota(jnp.int32, (2, 4), 1) + 2 * lax.broadcasted_iota(jnp.int32, (2, 4), 0)
-    mine = lax.dynamic_slice_in_dim(offsets, sub * 4, 4, 1)
-    code = (jnp.sum(jnp.left_shift(mine, shifts)) | (sub << 24)).reshape(1)
     w_cols = lax.dynamic_slice_in_dim(w_out, sub * cols, cols, 1)
 
     def along_z(value, up, down):
@@ -349,25 +357,27 @@
 
     smem_offsets = pltpu.SMEM(offsets.shape, jnp.int32)
     q_t, k_t, v_t = q_heads.T, k_heads.T, v_heads.T
-    near_q, w_cols = lax.optimization_barrier((q_t, w_cols))
-    kv_mid, kv_wide = call(
+    kv_mid, kv_wide, own_code = call(
         prep_kernel, "aaa",
-        [((mid, 384), BF16), ((wide, 384), BF16)],
+        [((mid, 384), BF16), ((wide, 384), BF16), ((1,), jnp.int32)],
         [((cols, rows), BF16)] * 2 + [smem_offsets] + [((rows, 128), F32)] * 3 + [pltpu.SemaphoreType.DMA((3,))],
         2e8, 60,
     )(offsets, k_t, v_t)
 
+    code = own_code | (sub << 24)
+    near_q, w_cols, code = lax.optimization_barrier((q_t, w_cols, code))
     four = n_chips // 4
     kv_both = flipped(kv_wide, 1)
     far_mid = flipped(kv_mid, 2)
     own_pair = jnp.concatenate([kv_wide, kv_both], axis=0)
     far4 = along_z(own_pair, four, -four)
     acc, q_mid, q_wide = call(
-        near_kernel, "ssvvv",
+        near_kernel, "asvvv",
         [((2, rows, 128), F32), ((4 * mid, 256), BF16), ((4 * wide, 256), BF16)],
-        [((rows, 256), BF16), ((256, rows), BF16), ((256, rows), BF16)] + [((rows, 128), F32)] * 2,
+        [((rows, 256), BF16), ((256, rows), BF16), ((256, rows), BF16)] + [((rows, 128), F32)] * 2
+        + [smem_offsets, pltpu.SemaphoreType.DMA],
         4e9, 28,
-    )(code, valid, near_q, k_t, v_t)
+    )(offsets, valid, near_q, k_t, v_t)
     far_mid, acc = lax.optimization_barrier((far_mid, acc))
 
     swap_mid = flipped(jnp.concatenate([kv_mid, far_mid], axis=0), 1)
@@ -400,12 +410,13 @@
     acc_wide = wide_part(((0, False), (0, True)), acc_wide, (early, early_other))
     acc_wide = wide_part(((1, False),), acc_wide, (late,))
     attn_wide = wide_part(((1, True),), acc_wide, (late_other,), last=True)
+    (w_blocks,) = call(weights_kernel, "v", [((2, 4 * 256, 256), BF16)], [], 1e7)(w_cols)
     wides = [along_x(attn_wide, s) for s in (1, n_sub - 1, 2)]
     (out,) = call(
         final_kernel, "asv" + "v" * 8, [((cols, rows), BF16)],
         [((rows, 128), F32)] * 2
-        + [((2, 4 * 256, 256), BF16), smem_offsets, pltpu.SemaphoreType.DMA], 1e9,
-    )(offsets, valid, w_cols, attn, *attns, attn_wide, *wides)
+        + [smem_offsets, pltpu.SemaphoreType.DMA], 1e9,
+    )(offsets, valid, w_blocks, attn, *attns, attn_wide, *wides)
     return out.T
 
 

time: 91.3 us -> 90.4 us (level)
    pallas_call x2 -> x3, Pallas kernels: 8.65 us -> 8.8 us  [the longest x1 6.14 us: local(): call(near_kernel, 'asvvv', [((2, rows, 128), F32), ((4 * mid, 256), BF16)...]
  transfers between devices with their start and end apart: 16 -> 16, of which waited for: 5 -> 5; matrix products, arithmetic and copies ran while one was open for 1% -> 0% of each run, Pallas kernels for 14% -> 14%
where the time goes in v3:
time: 90.4 us; the launch traced here: 89.3 us
  starting transfers between devices  52.1 us (58%)
  Pallas kernels  17.7 us (20%)
  waiting for transfers between devices  17.4 us (19%)
  between operations  1.72 us (2%)
    ppermute x5, starting transfers between devices, flipped(): return lax.ppermute(value, 'seq', [(i, i ^ mask) for i in range(n_seq)])  26.5 us
    ppermute x5, starting transfers between devices, along_z(): return lax.ppermute(value, 'seq', pairs)  14.4 us
    ppermute x6, starting transfers between devices, along_x(): lax.ppermute(value, 'sub', [(i, (i + step) % n_sub) for i in range(n_sub)])  11.1 us
    ppermute x6, waiting for transfers between devices, along_x(): lax.ppermute(value, 'sub', [(i, (i + step) % n_sub) for i in range(n_sub)])  9.36 us
    ppermute x5, waiting for transfers between devices, along_z(): return lax.ppermute(value, 'seq', pairs)  8.06 us
    pallas_call x1, Pallas kernels, local(): call(near_kernel, 'asvvv', [((2, rows, 128), F32), ((4 * mid, 256), BF16)...  6.14 us
    pallas_call x3, Pallas kernels, wide_part(): call(functools.partial(wide_kernel, rows, n_chips, plan, last), 'ssvv' +...  3.15 us
    pallas_call x1, Pallas kernels, local(): call(functools.partial(middle_kernel, rows), 'ssvvvvv', [((rows + rows //...  2.97 us
  transfers between devices with their start and end apart: 16, of which 5 were waited for; matrix products, arithmetic and copies ran while one was open for 0% of the time, Pallas kernels for 14%

profile of v3, /device:TPU:33, one launch (start us, length us, event | category | flops | bytes accessed | tf_op | source)
XLA Modules:
  0.0 89.3 jit_solution(3548762045537679319)
XLA Ops:
  0.0 0.0 copy-start
  0.0 0.0 copy-start.4
  0.0 0.0 copy-start.1
  0.0 0.0 copy-start.2
  0.0 0.0 copy-start.5
  0.0 2.5 %shard_map.64 = (bf16[256,384]{1,0:T(8,128)(2,1)}, bf16[64,384]{1,0:T(8,128)(2,1)}, s32[1]{0:T(128)}) custom-call(s32[2,16]{1,0:T(2,128)} %offs_hbm.5, bf16[192,1024]{1,0:T(8,128)(2,1)} %bitcast.5, bf16[192,1024]{1,0:T(8,128)(2,1)} %bitcast.7), custom_call_target="tpu_custom_call" | custom-call | flops 200000000 | bytes 2097152 | tf_op jit(solution)/shard_map/pallas_call | solution.py:360
  2.5 3.4 %collective-permute-start = (bf16[256,384]{1,0:T(8,128)(2,1)}, bf16[256,384]{1,0:T(8,128)(2,1)S(1)}, u32[]{:S(2)}, u32[]{:S(2)}) collective-permute-start(bf16[256,384]{1,0:T(8,128)(2,1)} %get-tuple-element.21.own_ref), channel_id=1, source_target_pairs={{0,8},{4,12},{8,0},{12,4},{16,24},{20,28},{24,16},{28,20},{32,40},... | collective-permute-start | bytes 589832 | tf_op jit(solution)/shard_map/ppermute | solution.py:353
  6.0 17.2 %collective-permute-start.5 = (bf16[64,384]{1,0:T(8,128)(2,1)}, bf16[64,384]{1,0:T(8,128)(2,1)S(1)}, u32[]{:S(2)}, u32[]{:S(2)}) collective-permute-start(bf16[64,384]{1,0:T(8,128)(2,1)} %get-tuple-element.30), channel_id=1, source_target_pairs={{0,4},{4,0},{8,12},{12,8},{16,20},{20,16},{24,28},{28,24},{32,36},... | collective-permute-start | bytes 147464 | tf_op jit(solution)/shard_map/ppermute | solution.py:353
  23.9 0.0 copy-done
  23.9 0.2 constant_dynamic-slice_fusion.w_ref
  24.7 0.0 copy-done.4
  24.8 0.0 copy-done.1
  24.8 0.0 copy-done.2
  24.8 0.0 copy-done.5
  24.8 0.0 copy-start.6
  24.8 6.1 %shard_map.66 = (f32[2,1024,128]{2,1,0:T(8,128)S(1)}, bf16[1024,256]{1,0:T(8,128)(2,1)S(1)}, bf16[256,256]{1,0:T(8,128)(2,1)S(1)}) custom-call(s32[2,16]{1,0:T(2,128)S(1)} %copy-done.4, s32[1]{0:T(128)S(6)} %copy.13.valid, bf16[192,1024]{1,0:T(8,128)(2,1)S(1)} %bitcast.9, bf16[192,1024]{1,0:T(8,128)(2,1)S(1)} %bitcast.6, bf16[192,1024]{1,0:T(8,128)(2,1)S(1)} %bitcast.8), custom_call_target="tpu_custom_call" | custom-call | flops 4000000000 | bytes 2097152 | tf_op jit(solution)/shard_map/pallas_call | solution.py:374
  30.9 0.0 copy-start.3
  31.0 0.0 collective-permute-done.5
  31.0 0.0 copy-done.6
  31.0 3.7 %collective-permute-start.6 = (bf16[128,384]{1,0:T(8,128)(2,1)S(1)}, bf16[128,384]{1,0:T(8,128)(2,1)S(1)}, u32[]{:S(2)}, u32[]{:S(2)}) collective-permute-start(bf16[128,384]{1,0:T(8,128)(2,1)S(1)} %pad_maximum_fusion.2), channel_id=1, source_target_pairs={{0,32},{4,100},{8,40},{12,108},{16,48},{20,116},{24,56},{28,124},{... | collective-permute-start | bytes 294920 | tf_op jit(solution)/shard_map/ppermute | solution.py:350
  34.7 4.1 %collective-permute-done.6 = bf16[128,384]{1,0:T(8,128)(2,1)S(1)} collective-permute-done((bf16[128,384]{1,0:T(8,128)(2,1)S(1)}, bf16[128,384]{1,0:T(8,128)(2,1)S(1)}, u32[]{:S(2)}, u32[]{:S(2)}) %collective-permute-start.6) | collective-permute-done | bytes 98336 | tf_op jit(solution)/shard_map/ppermute | solution.py:350
  38.8 4.2 %collective-permute-start.7 = (bf16[64,384]{1,0:T(8,128)(2,1)S(1)}, bf16[64,384]{1,0:T(8,128)(2,1)S(1)}, u32[]{:S(2)}, u32[]{:S(2)}) collective-permute-start(bf16[64,384]{1,0:T(8,128)(2,1)S(1)} %slice.4), channel_id=1, source_target_pairs={{0,32},{4,100},{8,40},{12,108},{16,48},{20,116},{24,56},{28,124},{... | collective-permute-start | bytes 147464 | tf_op jit(solution)/shard_map/ppermute | solution.py:350
  43.1 2.1 %collective-permute-start.8 = (bf16[256,384]{1,0:T(8,128)(2,1)S(1)}, bf16[256,384]{1,0:T(8,128)(2,1)S(1)}, u32[]{:S(2)}, u32[]{:S(2)}) collective-permute-start(bf16[256,384]{1,0:T(8,128)(2,1)S(1)} %pad_maximum_fusion.1), channel_id=1, source_target_pairs={{0,16},{4,116},{8,24},{12,124},{16,32},{20,4},{24,40},{28,12},{32,... | collective-permute-start | bytes 589832 | tf_op jit(solution)/shard_map/ppermute | solution.py:350
  45.1 0.5 collective-permute-done.7
  45.7 0.0 collective-permute-done.far_ref
  45.7 1.8 %collective-permute-start.10 = (bf16[256,384]{1,0:T(8,128)(2,1)S(1)}, bf16[256,384]{1,0:T(8,128)(2,1)S(1)}, u32[]{:S(2)}, u32[]{:S(2)}) collective-permute-start(bf16[256,384]{1,0:T(8,128)(2,1)S(1)} %get-tuple-element.33), channel_id=1, source_target_pairs={{0,8},{4,12},{8,16},{12,20},{16,24},{20,28},{24,32},{28,36},{32,40... | collective-permute-start | bytes 589832 | tf_op jit(solution)/shard_map/ppermute | solution.py:350
  47.4 0.0 copy-done.3
  47.5 4.0 %collective-permute-start.1 = (bf16[512,384]{1,0:T(8,128)(2,1)S(1)}, bf16[512,384]{1,0:T(8,128)(2,1)S(1)}, u32[]{:S(2)}, u32[]{:S(2)}) collective-permute-start(bf16[512,384]{1,0:T(8,128)(2,1)S(1)} %pad_maximum_fusion), channel_id=1, source_target_pairs={{0,4},{4,0},{8,12},{12,8},{16,20},{20,16},{24,28},{28,24},{32,36},... | collective-permute-start | bytes 1179656 | tf_op jit(solution)/shard_map/ppermute | solution.py:353
  51.5 2.6 %collective-permute-start.11 = (bf16[256,384]{1,0:T(8,128)(2,1)S(1)}, bf16[256,384]{1,0:T(8,128)(2,1)S(1)}, u32[]{:S(2)}, u32[]{:S(2)}) collective-permute-start(bf16[256,384]{1,0:T(8,128)(2,1)S(1)} %get-tuple-element.33), channel_id=1, source_target_pairs={{0,120},{4,124},{8,0},{12,4},{16,8},{20,12},{24,16},{28,20},{32,24... | collective-permute-start | bytes 589832 | tf_op jit(solution)/shard_map/ppermute | solution.py:350
  54.1 0.0 collective-permute-done.8
  54.2 0.5 collective-permute-start.9
  54.7 0.0 collective-permute-done.10
  54.7 3.5 %collective-permute-done.11 = bf16[256,384]{1,0:T(8,128)(2,1)S(1)} collective-permute-done((bf16[256,384]{1,0:T(8,128)(2,1)S(1)}, bf16[256,384]{1,0:T(8,128)(2,1)S(1)}, u32[]{:S(2)}, u32[]{:S(2)}) %collective-permute-start.11) | collective-permute-done | bytes 196640 | tf_op jit(solution)/shard_map/ppermute | solution.py:350
  58.3 1.3 %collective-permute-start.12 = (bf16[512,384]{1,0:T(8,128)(2,1)S(1)}, bf16[512,384]{1,0:T(8,128)(2,1)S(1)}, u32[]{:S(2)}, u32[]{:S(2)}) collective-permute-start(bf16[512,384]{1,0:T(8,128)(2,1)S(1)} %constant_dynamic-update-slice_fusion.7.refs_0_), channel_id=1, source_target_pairs={{0,4},{4,0},{8,12},{12,8},{16,20},{20,16},{24,28},{28,24},{32,36},... | collective-permute-start | bytes 1179656 | tf_op jit(solution)/shard_map/ppermute | solution.py:353
  59.6 0.0 collective-permute-done.1.swap_ref
  59.6 3.0 %shard_map.67 = (bf16[1536,128]{1,0:T(8,128)(2,1)S(1)}, f32[2,64,128]{2,1,0:T(8,128)S(1)}) custom-call(s32[1]{0:T(128)S(6)} %or.7.code, s32[1]{0:T(128)S(6)} %copy.13.valid, f32[2,1024,128]{2,1,0:T(8,128)S(1)} %get-tuple-element.24.acc_ref, bf16[1024,256]{1,0:T(8,128)(2,1)S(1)} %get-tuple-element.25.qm_ref, bf16[256,384]{1,0:T(8,128)(2,1)S(1)} %copy-done.3, ...), custom_call_target="tpu_custom_call" | custom-call | flops 1000000000 | bytes 2097152 | tf_op jit(solution)/shard_map/pallas_call | solution.py:389
  62.6 1.7 %collective-permute-start.2 = (bf16[1536,128]{1,0:T(8,128)(2,1)S(1)}, bf16[1536,128]{1,0:T(8,128)(2,1)S(1)}, u32[]{:S(2)}, u32[]{:S(2)}) collective-permute-start(bf16[1536,128]{1,0:T(8,128)(2,1)S(1)} %get-tuple-element.27.a0_ref), channel_id=1, source_target_pairs={{0,1},{1,2},{2,3},{3,0},{4,5},{5,6},{6,7},{7,4},{8,9},{9,10},{10,1... | collective-permute-start | bytes 1179656 | tf_op jit(solution)/shard_map/ppermute | solution.py:356
  64.2 1.7 %collective-permute-start.3 = (bf16[1536,128]{1,0:T(8,128)(2,1)S(1)}, bf16[1536,128]{1,0:T(8,128)(2,1)S(1)}, u32[]{:S(2)}, u32[]{:S(2)}) collective-permute-start(bf16[1536,128]{1,0:T(8,128)(2,1)S(1)} %get-tuple-element.27.a0_ref), channel_id=1, source_target_pairs={{0,3},{1,0},{2,1},{3,2},{4,7},{5,4},{6,5},{7,6},{8,11},{9,8},{10,9... | collective-permute-start | bytes 1179656 | tf_op jit(solution)/shard_map/ppermute | solution.py:356
  65.9 1.5 %collective-permute-start.4 = (bf16[1536,128]{1,0:T(8,128)(2,1)S(1)}, bf16[1536,128]{1,0:T(8,128)(2,1)S(1)}, u32[]{:S(2)}, u32[]{:S(2)}) collective-permute-start(bf16[1536,128]{1,0:T(8,128)(2,1)S(1)} %get-tuple-element.27.a0_ref), channel_id=1, source_target_pairs={{0,2},{1,3},{2,0},{3,1},{4,6},{5,7},{6,4},{7,5},{8,10},{9,11},{10,... | collective-permute-start | bytes 1179656 | tf_op jit(solution)/shard_map/ppermute | solution.py:356
  67.4 0.0 collective-permute-done.9.refs_1_
  67.4 1.2 %shard_map.68.accw_ref = f32[2,64,128]{2,1,0:T(8,128)S(1)} custom-call(s32[1]{0:T(128)S(6)} %or.7.code, s32[1]{0:T(128)S(6)} %copy.13.valid, bf16[256,256]{1,0:T(8,128)(2,1)S(1)} %get-tuple-element.28.qw_ref, f32[2,64,128]{2,1,0:T(8,128)S(1)} %get-tuple-element.29.accw_ref, bf16[512,384]{1,0:T(8,128)(2,1)S(1)} %constant_dynamic-update-slice_fusion.refs_0_, ...), custom_call_target="tpu_custom_call" | custom-call | flops 500000000 | bytes 2097152 | tf_op jit(solution)/shard_map/pallas_call | solution.py:399
  68.6 0.9 %shard_map.69.accw_ref = f32[2,64,128]{2,1,0:T(8,128)S(1)} custom-call(s32[1]{0:T(128)S(6)} %or.7.code, s32[1]{0:T(128)S(6)} %copy.13.valid, bf16[256,256]{1,0:T(8,128)(2,1)S(1)} %get-tuple-element.28.qw_ref, f32[2,64,128]{2,1,0:T(8,128)S(1)} %shard_map.68.accw_ref, bf16[512,384]{1,0:T(8,128)(2,1)S(1)} %constant_dynamic-update-slice_fusion.7.refs_0_), custom_call_target="tpu_custom_call" | custom-call | flops 500000000 | bytes 2097152 | tf_op jit(solution)/shard_map/pallas_call | solution.py:399
  69.5 0.0 collective-permute-done.12.refs_0_
  69.5 1.1 %shard_map.70.b0_ref = bf16[96,128]{1,0:T(8,128)(2,1)S(1)} custom-call(s32[1]{0:T(128)S(6)} %or.7.code, s32[1]{0:T(128)S(6)} %copy.13.valid, bf16[256,256]{1,0:T(8,128)(2,1)S(1)} %get-tuple-element.28.qw_ref, f32[2,64,128]{2,1,0:T(8,128)S(1)} %shard_map.69.accw_ref, bf16[512,384]{1,0:T(8,128)(2,1)S(1)} %collective-permute-done.12.refs_0_), custom_call_target="tpu_custom_call" | custom-call | flops 500000000 | bytes 2097152 | tf_op jit(solution)/shard_map/pallas_call | solution.py:399
  70.6 0.5 collective-permute-start.13
  71.1 2.3 %collective-permute-start.14 = (bf16[96,128]{1,0:T(8,128)(2,1)S(1)}, bf16[96,128]{1,0:T(8,128)(2,1)S(1)}, u32[]{:S(2)}, u32[]{:S(2)}) collective-permute-start(bf16[96,128]{1,0:T(8,128)(2,1)S(1)} %shard_map.70.b0_ref), channel_id=1, source_target_pairs={{0,3},{1,0},{2,1},{3,2},{4,7},{5,4},{6,5},{7,6},{8,11},{9,8},{10,9... | collective-permute-start | bytes 73736 | tf_op jit(solution)/shard_map/ppermute | solution.py:356
  73.3 8.3 %collective-permute-done.13.b1_ref = bf16[96,128]{1,0:T(8,128)(2,1)S(1)} collective-permute-done((bf16[96,128]{1,0:T(8,128)(2,1)S(1)}, bf16[96,128]{1,0:T(8,128)(2,1)S(1)}, u32[]{:S(2)}, u32[]{:S(2)}) %collective-permute-start.13) | collective-permute-done | bytes 24608 | tf_op jit(solution)/shard_map/ppermute | solution.py:356
  81.6 3.5 %collective-permute-start.15 = (bf16[96,128]{1,0:T(8,128)(2,1)S(1)}, bf16[96,128]{1,0:T(8,128)(2,1)S(1)}, u32[]{:S(2)}, u32[]{:S(2)}) collective-permute-start(bf16[96,128]{1,0:T(8,128)(2,1)S(1)} %shard_map.70.b0_ref), channel_id=1, source_target_pairs={{0,2},{1,3},{2,0},{3,1},{4,6},{5,7},{6,4},{7,5},{8,10},{9,11},{10,... | collective-permute-start | bytes 73736 | tf_op jit(solution)/shard_map/ppermute | solution.py:356
  85.2 0.2 shard_map.65.wp
  85.4 0.0 collective-permute-done.14.b2_ref
  85.4 1.0 %collective-permute-done.15.b3_ref = bf16[96,128]{1,0:T(8,128)(2,1)S(1)} collective-permute-done((bf16[96,128]{1,0:T(8,128)(2,1)S(1)}, bf16[96,128]{1,0:T(8,128)(2,1)S(1)}, u32[]{:S(2)}, u32[]{:S(2)}) %collective-permute-start.15) | collective-permute-done | bytes 24608 | tf_op jit(solution)/shard_map/ppermute | solution.py:356
  86.4 0.0 collective-permute-done.2.a1_ref
  86.4 0.0 collective-permute-done.3.a2_ref
  86.4 0.0 collective-permute-done.4.a3_ref
  86.4 2.8 %shard_map.71 = bf16[192,1024]{1,0:T(8,128)(2,1)} custom-call(s32[2,16]{1,0:T(2,128)S(1)} %copy-done.4, s32[1]{0:T(128)S(6)} %copy.13.valid, bf16[2,1024,256]{2,1,0:T(8,128)(2,1)S(1)} %shard_map.65.wp, bf16[1536,128]{1,0:T(8,128)(2,1)S(1)} %get-tuple-element.27.a0_ref, bf16[1536,128]{1,0:T(8,128)(2,1)S(1)} %collective-permute-done.2.a1_ref, ...), custom_call_target="tpu_custom_call" | custom-call | flops 1000000000 | bytes 2097152 | tf_op jit(solution)/shard_map/pallas_call | solution.py:415
  (10 shorter events, 0.2 us)
Async XLA Ops:
  0.0 23.9 %copy-start = (bf16[768,768]{1,0:T(8,128)(2,1)S(1)}, bf16[768,768]{1,0:T(8,128)(2,1)}, u32[]{:S(2)}) copy-start(bf16[768,768]{1,0:T(8,128)(2,1)} %param.9) | copy-start | bytes 3538948
  0.0 24.7 %copy-start.4 = (s32[2,16]{1,0:T(2,128)S(1)}, s32[2,16]{1,0:T(2,128)}, u32[]{:S(2)}) copy-start(s32[2,16]{1,0:T(2,128)} %offs_hbm.5) | copy-start | bytes 388
  0.0 24.8 %copy-start.1 = (bf16[1024,192]{0,1:T(8,128)(2,1)S(1)}, bf16[1024,192]{0,1:T(8,128)(2,1)}, u32[]{:S(2)}) copy-start(bf16[1024,192]{0,1:T(8,128)(2,1)} %param.7) | copy-start | bytes 1179652
  0.0 24.8 %copy-start.2 = (bf16[1024,192]{0,1:T(8,128)(2,1)S(1)}, bf16[1024,192]{0,1:T(8,128)(2,1)}, u32[]{:S(2)}) copy-start(bf16[1024,192]{0,1:T(8,128)(2,1)} %param.8) | copy-start | bytes 1179652
  0.0 24.8 %copy-start.5 = (bf16[1024,192]{0,1:T(8,128)(2,1)S(1)}, bf16[1024,192]{0,1:T(8,128)(2,1)}, u32[]{:S(2)}) copy-start(bf16[1024,192]{0,1:T(8,128)(2,1)} %param.6) | copy-start | bytes 1179652
  2.5 43.1 %collective-permute-start = (bf16[256,384]{1,0:T(8,128)(2,1)}, bf16[256,384]{1,0:T(8,128)(2,1)S(1)}, u32[]{:S(2)}, u32[]{:S(2)}) collective-permute-start(bf16[256,384]{1,0:T(8,128)(2,1)} %get-tuple-element.21.own_ref), channel_id=1, source_target_pairs={{0,8},{4,12},{8,0},{12,4},{16,24},{20,28},{24,16},{28,20},{32,40},... | collective-permute-start | bytes 589832 | tf_op jit(solution)/shard_map/ppermute | solution.py:353
  6.0 25.0 %collective-permute-start.5 = (bf16[64,384]{1,0:T(8,128)(2,1)}, bf16[64,384]{1,0:T(8,128)(2,1)S(1)}, u32[]{:S(2)}, u32[]{:S(2)}) collective-permute-start(bf16[64,384]{1,0:T(8,128)(2,1)} %get-tuple-element.30), channel_id=1, source_target_pairs={{0,4},{4,0},{8,12},{12,8},{16,20},{20,16},{24,28},{28,24},{32,36},... | collective-permute-start | bytes 147464 | tf_op jit(solution)/shard_map/ppermute | solution.py:353
  24.8 6.2 %copy-start.6 = (bf16[64,384]{1,0:T(8,128)(2,1)S(1)}, bf16[64,384]{1,0:T(8,128)(2,1)}, u32[]{:S(2)}) copy-start(bf16[64,384]{1,0:T(8,128)(2,1)} %get-tuple-element.30) | copy-start | bytes 147460
  30.9 16.5 %copy-start.3 = (bf16[256,384]{1,0:T(8,128)(2,1)S(1)}, bf16[256,384]{1,0:T(8,128)(2,1)}, u32[]{:S(2)}) copy-start(bf16[256,384]{1,0:T(8,128)(2,1)} %get-tuple-element.21.own_ref) | copy-start | bytes 589828
  31.0 7.8 %collective-permute-start.6 = (bf16[128,384]{1,0:T(8,128)(2,1)S(1)}, bf16[128,384]{1,0:T(8,128)(2,1)S(1)}, u32[]{:S(2)}, u32[]{:S(2)}) collective-permute-start(bf16[128,384]{1,0:T(8,128)(2,1)S(1)} %pad_maximum_fusion.2), channel_id=1, source_target_pairs={{0,32},{4,100},{8,40},{12,108},{16,48},{20,116},{24,56},{28,124},{... | collective-permute-start | bytes 294920 | tf_op jit(solution)/shard_map/ppermute | solution.py:350
  38.8 6.8 %collective-permute-start.7 = (bf16[64,384]{1,0:T(8,128)(2,1)S(1)}, bf16[64,384]{1,0:T(8,128)(2,1)S(1)}, u32[]{:S(2)}, u32[]{:S(2)}) collective-permute-start(bf16[64,384]{1,0:T(8,128)(2,1)S(1)} %slice.4), channel_id=1, source_target_pairs={{0,32},{4,100},{8,40},{12,108},{16,48},{20,116},{24,56},{28,124},{... | collective-permute-start | bytes 147464 | tf_op jit(solution)/shard_map/ppermute | solution.py:350
  43.1 11.1 %collective-permute-start.8 = (bf16[256,384]{1,0:T(8,128)(2,1)S(1)}, bf16[256,384]{1,0:T(8,128)(2,1)S(1)}, u32[]{:S(2)}, u32[]{:S(2)}) collective-permute-start(bf16[256,384]{1,0:T(8,128)(2,1)S(1)} %pad_maximum_fusion.1), channel_id=1, source_target_pairs={{0,16},{4,116},{8,24},{12,124},{16,32},{20,4},{24,40},{28,12},{32,... | collective-permute-start | bytes 589832 | tf_op jit(solution)/shard_map/ppermute | solution.py:350
  45.7 9.0 %collective-permute-start.10 = (bf16[256,384]{1,0:T(8,128)(2,1)S(1)}, bf16[256,384]{1,0:T(8,128)(2,1)S(1)}, u32[]{:S(2)}, u32[]{:S(2)}) collective-permute-start(bf16[256,384]{1,0:T(8,128)(2,1)S(1)} %get-tuple-element.33), channel_id=1, source_target_pairs={{0,8},{4,12},{8,16},{12,20},{16,24},{20,28},{24,32},{28,36},{32,40... | collective-permute-start | bytes 589832 | tf_op jit(solution)/shard_map/ppermute | solution.py:350
  47.5 12.1 %collective-permute-start.1 = (bf16[512,384]{1,0:T(8,128)(2,1)S(1)}, bf16[512,384]{1,0:T(8,128)(2,1)S(1)}, u32[]{:S(2)}, u32[]{:S(2)}) collective-permute-start(bf16[512,384]{1,0:T(8,128)(2,1)S(1)} %pad_maximum_fusion), channel_id=1, source_target_pairs={{0,4},{4,0},{8,12},{12,8},{16,20},{20,16},{24,28},{28,24},{32,36},... | collective-permute-start | bytes 1179656 | tf_op jit(solution)/shard_map/ppermute | solution.py:353
  51.5 6.7 %collective-permute-start.11 = (bf16[256,384]{1,0:T(8,128)(2,1)S(1)}, bf16[256,384]{1,0:T(8,128)(2,1)S(1)}, u32[]{:S(2)}, u32[]{:S(2)}) collective-permute-start(bf16[256,384]{1,0:T(8,128)(2,1)S(1)} %get-tuple-element.33), channel_id=1, source_target_pairs={{0,120},{4,124},{8,0},{12,4},{16,8},{20,12},{24,16},{28,20},{32,24... | collective-permute-start | bytes 589832 | tf_op jit(solution)/shard_map/ppermute | solution.py:350
  54.2 13.2 %collective-permute-start.9 = (bf16[512,384]{1,0:T(8,128)(2,1)S(1)}, bf16[512,384]{1,0:T(8,128)(2,1)S(1)}, u32[]{:S(2)}, u32[]{:S(2)}) collective-permute-start(bf16[512,384]{1,0:T(8,128)(2,1)S(1)} %constant_dynamic-update-slice_fusion.refs_0_), channel_id=1, source_target_pairs={{0,4},{4,0},{8,12},{12,8},{16,20},{20,16},{24,28},{28,24},{32,36},... | collective-permute-start | bytes 1179656 | tf_op jit(solution)/shard_map/ppermute | solution.py:353
  58.3 11.2 %collective-permute-start.12 = (bf16[512,384]{1,0:T(8,128)(2,1)S(1)}, bf16[512,384]{1,0:T(8,128)(2,1)S(1)}, u32[]{:S(2)}, u32[]{:S(2)}) collective-permute-start(bf16[512,384]{1,0:T(8,128)(2,1)S(1)} %constant_dynamic-update-slice_fusion.7.refs_0_), channel_id=1, source_target_pairs={{0,4},{4,0},{8,12},{12,8},{16,20},{20,16},{24,28},{28,24},{32,36},... | collective-permute-start | bytes 1179656 | tf_op jit(solution)/shard_map/ppermute | solution.py:353
  62.6 23.8 %collective-permute-start.2 = (bf16[1536,128]{1,0:T(8,128)(2,1)S(1)}, bf16[1536,128]{1,0:T(8,128)(2,1)S(1)}, u32[]{:S(2)}, u32[]{:S(2)}) collective-permute-start(bf16[1536,128]{1,0:T(8,128)(2,1)S(1)} %get-tuple-element.27.a0_ref), channel_id=1, source_target_pairs={{0,1},{1,2},{2,3},{3,0},{4,5},{5,6},{6,7},{7,4},{8,9},{9,10},{10,1... | collective-permute-start | bytes 1179656 | tf_op jit(solution)/shard_map/ppermute | solution.py:356
  64.2 22.2 %collective-permute-start.3 = (bf16[1536,128]{1,0:T(8,128)(2,1)S(1)}, bf16[1536,128]{1,0:T(8,128)(2,1)S(1)}, u32[]{:S(2)}, u32[]{:S(2)}) collective-permute-start(bf16[1536,128]{1,0:T(8,128)(2,1)S(1)} %get-tuple-element.27.a0_ref), channel_id=1, source_target_pairs={{0,3},{1,0},{2,1},{3,2},{4,7},{5,4},{6,5},{7,6},{8,11},{9,8},{10,9... | collective-permute-start | bytes 1179656 | tf_op jit(solution)/shard_map/ppermute | solution.py:356
  65.9 20.5 %collective-permute-start.4 = (bf16[1536,128]{1,0:T(8,128)(2,1)S(1)}, bf16[1536,128]{1,0:T(8,128)(2,1)S(1)}, u32[]{:S(2)}, u32[]{:S(2)}) collective-permute-start(bf16[1536,128]{1,0:T(8,128)(2,1)S(1)} %get-tuple-element.27.a0_ref), channel_id=1, source_target_pairs={{0,2},{1,3},{2,0},{3,1},{4,6},{5,7},{6,4},{7,5},{8,10},{9,11},{10,... | collective-permute-start | bytes 1179656 | tf_op jit(solution)/shard_map/ppermute | solution.py:356
  70.6 11.1 %collective-permute-start.13 = (bf16[96,128]{1,0:T(8,128)(2,1)S(1)}, bf16[96,128]{1,0:T(8,128)(2,1)S(1)}, u32[]{:S(2)}, u32[]{:S(2)}) collective-permute-start(bf16[96,128]{1,0:T(8,128)(2,1)S(1)} %shard_map.70.b0_ref), channel_id=1, source_target_pairs={{0,1},{1,2},{2,3},{3,0},{4,5},{5,6},{6,7},{7,4},{8,9},{9,10},{10,1... | collective-permute-start | bytes 73736 | tf_op jit(solution)/shard_map/ppermute | solution.py:356
  71.1 14.3 %collective-permute-start.14 = (bf16[96,128]{1,0:T(8,128)(2,1)S(1)}, bf16[96,128]{1,0:T(8,128)(2,1)S(1)}, u32[]{:S(2)}, u32[]{:S(2)}) collective-permute-start(bf16[96,128]{1,0:T(8,128)(2,1)S(1)} %shard_map.70.b0_ref), channel_id=1, source_target_pairs={{0,3},{1,0},{2,1},{3,2},{4,7},{5,4},{6,5},{7,6},{8,11},{9,8},{10,9... | collective-permute-start | bytes 73736 | tf_op jit(solution)/shard_map/ppermute | solution.py:356
  81.6 4.8 %collective-permute-start.15 = (bf16[96,128]{1,0:T(8,128)(2,1)S(1)}, bf16[96,128]{1,0:T(8,128)(2,1)S(1)}, u32[]{:S(2)}, u32[]{:S(2)}) collective-permute-start(bf16[96,128]{1,0:T(8,128)(2,1)S(1)} %shard_map.70.b0_ref), channel_id=1, source_target_pairs={{0,2},{1,3},{2,0},{3,1},{4,6},{5,7},{6,4},{7,5},{8,10},{9,11},{10,... | collective-permute-start | bytes 73736 | tf_op jit(solution)/shard_map/ppermute | solution.py:356
